TPU v7x, 8 devices: a whole 2x2x1 slice. The times are simulated.
8 devices in a mesh: dp: 4 (over z, y, x), cp: 2 (over core).
Axes of the slice: x: 2, y: 2, z: 1, core: 2. Of those that a mesh axis runs over, the one named last changes fastest.
Arguments:
- x_in: bfloat16 [32, 512, 2048], P('dp', 'cp')
- d_out: bfloat16 [32, 512, 2048], P('dp', 'cp')
- w_q: bfloat16 [2048, 32, 64], replicated
- w_k: bfloat16 [2048, 4, 64], replicated
- w_v: bfloat16 [2048, 4, 64], replicated
- w_o: bfloat16 [32, 64, 2048], replicated
- w_up: bfloat16 [2048, 5632], replicated
- w_down: bfloat16 [5632, 2048], replicated
Outputs:
- output 1: bfloat16 [32, 512, 2048], P('dp', 'cp')
- output 2: float32 [2048, 32, 64], replicated
- output 3: float32 [2048, 4, 64], replicated
- output 4: float32 [2048, 4, 64], replicated
- output 5: float32 [32, 64, 2048], replicated
- output 6: float32 [2048, 5632], replicated
- output 7: float32 [5632, 2048], replicated
All inputs are finite; a program needn't handle non-finite values.
Results may differ from a plain program's by a relative error of at most 0.02.
Values are sent between devices in bfloat16 or wider.
A program may use at most 1 GiB of HBM per device.

v0:
```python
import functools
import jax
import jax.numpy as jnp
from jax import lax
from jax.sharding import PartitionSpec as P

ROW_CONTRACT = (((0,), (0,)), ((), ()))
LAST_CONTRACT = (((1,), (1,)), ((), ()))


def solution(mesh):
    cp_size = mesh.shape['cp']
    grad_divisor = mesh.shape['dp'] * cp_size
    next_perm = [(source, (source + 1) % cp_size) for source in range(cp_size)]

    def pass_on(arrays):
        return lax.ppermute(arrays, 'cp', next_perm)

    def device_backward(x_in, d_out, w_q, w_k, w_v, w_o, w_up, w_down):
        batch_dev, seq_dev, model_width = x_in.shape
        kv_heads, head_dim = w_k.shape[1], w_k.shape[2]
        group_size = w_q.shape[1] // kv_heads
        head_count = kv_heads * group_size
        score_scale = head_dim ** -0.5
        row_count = batch_dev * seq_dev
        x_rows = x_in.reshape(row_count, model_width)

        def project(weight):
            product = jnp.einsum('nd,dhe->nhe', x_rows, weight, preferred_element_type=jnp.float32)
            return product.astype(jnp.bfloat16)

        q_loc = project(w_q).reshape(batch_dev, seq_dev, kv_heads, group_size, head_dim)
        k_loc = project(w_k).reshape(batch_dev, seq_dev, kv_heads, head_dim)
        v_loc = project(w_v).reshape(batch_dev, seq_dev, kv_heads, head_dim)

        def block_scores(k_block):
            return jnp.einsum('bqkgd,bpkd->bkgqp', q_loc, k_block, preferred_element_type=jnp.float32) * score_scale

        def forward_block(softmax_state, k_block, v_block):
            row_max, row_sum, out_acc = softmax_state
            scores = block_scores(k_block)
            new_max = jnp.maximum(row_max, jnp.max(scores, axis=-1))
            rescale = jnp.exp(row_max - new_max)
            block_weights = jnp.exp(scores - new_max[..., None])
            row_sum = row_sum * rescale + jnp.sum(block_weights, axis=-1)
            block_out = jnp.einsum('bkgqp,bpkd->bkgqd', block_weights.astype(jnp.bfloat16), v_block, preferred_element_type=jnp.float32)
            return new_max, row_sum, out_acc * rescale[..., None] + block_out

        stat_shape = (batch_dev, kv_heads, group_size, seq_dev)
        softmax_state = (jnp.full(stat_shape, -jnp.inf, jnp.float32), jnp.zeros(stat_shape, jnp.float32), jnp.zeros(stat_shape + (head_dim,), jnp.float32))
        softmax_state = forward_block(softmax_state, k_loc, v_loc)

        def forward_step(step, state):
            softmax_state, kv_blocks = state
            kv_blocks = pass_on(kv_blocks)
            return forward_block(softmax_state, kv_blocks[0], kv_blocks[1]), kv_blocks

        softmax_state = lax.fori_loop(0, cp_size - 1, forward_step, (softmax_state, (k_loc, v_loc)))[0]
        row_max, row_sum, out_acc = softmax_state
        attn_out = (out_acc / row_sum[..., None]).astype(jnp.bfloat16)
        log_norm = row_max + jnp.log(row_sum)

        w_o_heads = w_o.reshape(kv_heads, group_size, head_dim, model_width)
        out_proj = jnp.einsum('bkgqd,kgde->bqe', attn_out, w_o_heads, preferred_element_type=jnp.float32)
        hidden = (x_in.astype(jnp.float32) + out_proj).astype(jnp.bfloat16)
        hidden_rows = hidden.reshape(row_count, model_width)
        up_proj = jnp.dot(hidden_rows, w_up, preferred_element_type=jnp.float32)
        gelu_tanh = functools.partial(jax.nn.gelu, approximate=True)
        gated, gelu_vjp = jax.vjp(gelu_tanh, up_proj)
        gated = gated.astype(jnp.bfloat16)

        dout_rows = d_out.reshape(row_count, model_width)
        dw_down = lax.dot_general(gated, dout_rows, ROW_CONTRACT, preferred_element_type=jnp.float32)
        d_gated = lax.dot_general(dout_rows, w_down, LAST_CONTRACT, preferred_element_type=jnp.float32).astype(jnp.bfloat16)
        d_up = gelu_vjp(d_gated.astype(jnp.float32))[0].astype(jnp.bfloat16)
        dw_up = lax.dot_general(hidden_rows, d_up, ROW_CONTRACT, preferred_element_type=jnp.float32)
        d_hidden = dout_rows.astype(jnp.float32) + lax.dot_general(d_up, w_up, LAST_CONTRACT, preferred_element_type=jnp.float32)
        d_hidden = d_hidden.astype(jnp.bfloat16).reshape(batch_dev, seq_dev, model_width)
        dw_o = jnp.einsum('bkgqd,bqe->kgde', attn_out, d_hidden, preferred_element_type=jnp.float32).reshape(w_o.shape)
        d_attn = jnp.einsum('bqe,kgde->bkgqd', d_hidden, w_o_heads, preferred_element_type=jnp.float32).astype(jnp.bfloat16)
        row_delta = jnp.einsum('bkgqd,bkgqd->bkgq', d_attn, attn_out, preferred_element_type=jnp.float32)

        def backward_block(dq_acc, k_block, v_block, dk_acc, dv_acc):
            block_probs = jnp.exp(block_scores(k_block) - log_norm[..., None])
            probs_bf16 = block_probs.astype(jnp.bfloat16)
            dv_acc = dv_acc + jnp.einsum('bkgqp,bkgqd->bpkd', probs_bf16, d_attn, preferred_element_type=jnp.float32)
            d_probs = jnp.einsum('bkgqd,bpkd->bkgqp', d_attn, v_block, preferred_element_type=jnp.float32)
            d_scores = (block_probs * (d_probs - row_delta[..., None]) * score_scale).astype(jnp.bfloat16)
            dq_acc = dq_acc + jnp.einsum('bkgqp,bpkd->bqkgd', d_scores, k_block, preferred_element_type=jnp.float32)
            dk_acc = dk_acc + jnp.einsum('bkgqp,bqkgd->bpkd', d_scores, q_loc, preferred_element_type=jnp.float32)
            return dq_acc, dk_acc, dv_acc

        kv_zeros = jnp.zeros(k_loc.shape, jnp.float32)
        dq_acc, dk_acc, dv_acc = backward_block(jnp.zeros(q_loc.shape, jnp.float32), k_loc, v_loc, kv_zeros, kv_zeros)

        def backward_step(step, state):
            dq_acc, travelling = state
            k_block, v_block, dk_acc, dv_acc = pass_on(travelling)
            dq_acc, dk_acc, dv_acc = backward_block(dq_acc, k_block, v_block, dk_acc, dv_acc)
            return dq_acc, (k_block, v_block, dk_acc, dv_acc)

        dq_acc, travelling = lax.fori_loop(0, cp_size - 1, backward_step, (dq_acc, (k_loc, v_loc, dk_acc, dv_acc)))
        dk_acc, dv_acc = pass_on((travelling[2], travelling[3]))

        d_q = dq_acc.astype(jnp.bfloat16).reshape(row_count, head_count, head_dim)
        d_k = dk_acc.astype(jnp.bfloat16).reshape(row_count, kv_heads, head_dim)
        d_v = dv_acc.astype(jnp.bfloat16).reshape(row_count, kv_heads, head_dim)
        dw_q = jnp.einsum('nd,nhe->dhe', x_rows, d_q, preferred_element_type=jnp.float32)
        dw_k = jnp.einsum('nd,nhe->dhe', x_rows, d_k, preferred_element_type=jnp.float32)
        dw_v = jnp.einsum('nd,nhe->dhe', x_rows, d_v, preferred_element_type=jnp.float32)
        d_x = d_hidden.reshape(row_count, model_width).astype(jnp.float32)
        d_x = d_x + jnp.einsum('nhe,dhe->nd', d_q, w_q, preferred_element_type=jnp.float32)
        d_x = d_x + jnp.einsum('nhe,dhe->nd', d_k, w_k, preferred_element_type=jnp.float32)
        d_x = d_x + jnp.einsum('nhe,dhe->nd', d_v, w_v, preferred_element_type=jnp.float32)
        d_x = d_x.astype(jnp.bfloat16).reshape(batch_dev, seq_dev, model_width)
        summed = lax.psum((dw_q, dw_k, dw_v, dw_o, dw_up, dw_down), ('dp', 'cp'))
        return (d_x,) + tuple(part_sum / grad_divisor for part_sum in summed)

    act_spec = P('dp', 'cp', None)
    return jax.shard_map(device_backward, mesh=mesh, in_specs=(act_spec, act_spec, P(), P(), P(), P(), P(), P()), out_specs=(act_spec, P(), P(), P(), P(), P(), P()), check_vma=False)
```

profile of v0, /device:TPU:0, one launch (start us, length us, event | category | flops | bytes accessed | tf_op | source)
XLA Modules:
  0.0 2240.4 jit_solution(5902239141985605246)
XLA Ops:
  54.5 28.7 %bitcast_reduce_fusion.1 = (f32[8,4,8,256]{3,2,1,0:T(8,128)S(1)}, f32[8,4,256,256,8]{3,2,4,1,0:T(8,128)}) fusion(bf16[8,256,4,8,64]{1,0,4,3,2:T(8,128)(2,1)} %bitcast.283, bf16[8,256,4,64,1]{1,0,3,2,4:T(8,128)(2,1)S(1)} %bitcast.291), kind=kOutput, calls=%fused_computation.7 | convolution fusion | flops 2180972544 | bytes 76808192 | tf_op jit(solution)/shard_map/bqkgd,bpkd->bkgqp/dot_general | solution.py:37
  83.2 30.6 %fusion.22 = f32[8,4,8,256,64]{3,4,2,1,0:T(8,128)} fusion(f32[8,4,256,256,8]{3,2,4,1,0:T(8,128)} %get-tuple-element.71, f32[8,4,8,256]{3,2,1,0:T(8,128)S(1)} %get-tuple-element.70, bf16[8,256,4,64,1]{1,0,3,2,4:T(8,128)(2,1)S(1)} %bitcast.302), kind=kOutput, calls=%fused_computation.34 | convolution fusion | flops 2197815296 | bytes 85196800 | tf_op jit(solution)/shard_map/bkgqp,bpkd->bkgqd/dot_general | solution.py:46
  113.8 28.5 %bitcast_reduce_fusion = (f32[8,4,8,256]{3,2,1,0:T(8,128)S(1)}, f32[8,4,256,256,8]{3,2,4,1,0:T(8,128)}) fusion(bf16[8,256,4,8,64]{1,0,4,3,2:T(8,128)(2,1)} %bitcast.284, bf16[8,256,4,64]{1,3,2,0:T(8,128)(2,1)S(1)} %collective-permute-done), kind=kOutput, calls=%fused_computation.2 | convolution fusion | flops 2180972544 | bytes 76808192 | tf_op jit(solution)/shard_map/while/body/eval_jaxpr/bqkgd,bpkd->bkgqp/dot_general | solution.py:37
  143.0 41.8 %fusion.5 = (f32[8,4,8,256]{3,2,1,0:T(8,128)S(1)}, f32[8,4,8,256]{3,2,1,0:T(8,128)S(1)}) fusion(f32[8,4,256,256,8]{3,2,4,1,0:T(8,128)} %get-tuple-element.71, f32[8,4,8,256]{3,2,1,0:T(8,128)S(1)} %get-tuple-element.70, f32[8,4,8,256]{3,2,1,0:T(8,128)S(1)} %max.21, f32[8,4,256,256,8]{3,2,4,1,0:T(8,128)} %get-tuple-element.73), kind=kLoop, calls=%fused_computation.15 | loop fusion | flops 100532224 | bytes 135266304 | tf_op jit(solution)/shard_map/reduce_sum | solution.py:45
  185.7 37.3 %divide_convert_fusion = (bf16[8,4,8,256,64]{3,4,2,1,0:T(8,128)(2,1)}, f32[8,4,8,256,64]{3,4,2,1,0:T(8,128)}) fusion(f32[8,4,8,256,64]{3,4,2,1,0:T(8,128)} %fusion.22, f32[8,4,8,256]{3,2,1,0:T(8,128)S(1)} %get-tuple-element.56, f32[8,4,8,256]{3,2,1,0:T(8,128)S(1)} %get-tuple-element.57, f32[8,4,8,256]{3,2,1,0:T(8,128)S(1)} %get-tuple-element.69, ...), kind=kOutput, calls=%fused_computation.63 | convolution fusion | flops 2218786816 | bytes 111149056 | tf_op jit(solution)/shard_map/while/body/eval_jaxpr/bkgqp,bpkd->bkgqd/dot_general | solution.py:46
  223.0 24.4 %fusion.37 = bf16[8,256,2048]{2,1,0:T(8,128)(2,1)} fusion(bf16[8,256,2048]{2,1,0:T(8,128)(2,1)} %param.8, bf16[8,4,8,256,64]{3,4,2,1,0:T(8,128)(2,1)} %get-tuple-element.74, bf16[4,8,64,2048,1]{3,2,1,0,4:T(8,128)(2,1)} %bitcast.312), kind=kOutput, calls=%fused_computation.49 | convolution fusion | flops 17192452096 | bytes 33554432 | tf_op jit(solution)/shard_map/bkgqd,kgde->bqe/dot_general | solution.py:64
  247.3 58.3 %fusion.107 = f32[2048,5632]{1,0:T(8,128)} fusion(bf16[2048,2048]{1,0:T(8,128)(2,1)} %bitcast.321, bf16[2048,5632]{1,0:T(8,128)(2,1)} %param.14), kind=kOutput, calls=%fused_computation.132 | convolution fusion | flops 47244640256 | bytes 77594624 | tf_op jit(solution)/shard_map/dot_general | solution.py:67
  305.6 60.3 %fusion.32 = f32[5632,2048]{1,0:T(8,128)} fusion(bf16[2048,2048]{1,0:T(8,128)(2,1)} %bitcast.309, f32[2048,5632]{1,0:T(8,128)} %fusion.107), kind=kOutput, calls=%fused_computation.41 | convolution fusion | flops 47348449280 | bytes 100663296 | tf_op jit(solution)/shard_map/dot_general | solution.py:73
  365.9 92.1 %fusion.12 = bf16[2048,5632]{1,0:T(8,128)(2,1)} fusion(f32[2048,5632]{1,0:T(8,128)} %fusion.107, bf16[2048,2048]{1,0:T(8,128)(2,1)} %bitcast.310, bf16[5632,2048]{1,0:T(8,128)(2,1)} %param.15), kind=kOutput, calls=%fused_computation.24 | convolution fusion | flops 47498395648 | bytes 100663296 | tf_op jit(solution)/shard_map/dot_general | solution.py:74
  458.0 61.4 %add_convert_fusion.1 = bf16[2048,2048]{1,0:T(8,128)(2,1)S(1)} fusion(bf16[2048,2048]{1,0:T(8,128)(2,1)} %bitcast.311, bf16[2048,5632]{1,0:T(8,128)(2,1)} %fusion.12, bf16[2048,5632]{1,0:T(8,128)(2,1)} %param.14), kind=kOutput, calls=%fused_computation.62 | convolution fusion | flops 47257223168 | bytes 62914560 | tf_op jit(solution)/shard_map/dot_general | solution.py:77
  519.4 26.5 %fusion.42 = (f32[8,4,8,256]{3,2,1,0:T(8,128)}, bf16[8,256,4,8,64]{1,4,3,2,0:T(8,128)(2,1)}) fusion(bf16[8,4,8,256,64]{3,4,2,1,0:T(8,128)(2,1)} %get-tuple-element.74, bf16[8,256,2048,1,1]{2,1,4,3,0:T(8,128)(2,1)S(1)} %bitcast.297, bf16[4,8,64,2048,1]{3,2,1,0,4:T(8,128)(2,1)} %bitcast.313), kind=kOutput, calls=%fused_computation.60 | convolution fusion | flops 17200775168 | bytes 33816576 | tf_op jit(solution)/shard_map/bqe,kgde->bkgqd/dot_general | solution.py:80
  545.9 27.3 %fusion.66 = f32[8,256,4,64]{1,3,2,0:T(8,128)} fusion(f32[8,4,256,256,8]{3,2,4,1,0:T(8,128)} %get-tuple-element.71, f32[8,4,8,256]{3,2,1,0:T(8,128)S(1)} %copy-done.10, bf16[8,256,4,8,64]{1,4,3,2,0:T(8,128)(2,1)} %get-tuple-element.77), kind=kOutput, calls=%fused_computation.90 | convolution fusion | flops 2197815296 | bytes 77856768 | tf_op jit(solution)/shard_map/bkgqp,bkgqd->bpkd/dot_general | solution.py:86
  573.2 40.2 %multiply_convert_fusion.1 = bf16[8,4,8,256,256]{3,4,2,1,0:T(8,128)(2,1)} fusion(f32[8,4,256,256,8]{3,2,4,1,0:T(8,128)} %get-tuple-element.71, f32[8,4,8,256]{3,2,1,0:T(8,128)S(1)} %copy-done.22, f32[8,4,8,256]{3,2,1,0:T(8,128)S(1)} %copy-done.10, bf16[8,256,4,8,64]{1,4,3,2,0:T(8,128)(2,1)} %get-tuple-element.77, bf16[8,256,4,64,1]{1,0,3,2,4:T(8,128)(2,1)S(1)} %bitcast.303), kind=kOutput, calls=%fused_computation.11 | convolution fusion | flops 2248146944 | bytes 110624768 | tf_op jit(solution)/shard_map/bkgqd,bpkd->bkgqp/dot_general | solution.py:87
  632.6 22.0 fusion.86
  654.6 59.7 %fusion.110 = f32[2048,5632]{1,0:T(8,128)} fusion(bf16[2048,2048]{1,0:T(8,128)(2,1)} %bitcast.322, bf16[2048,5632]{1,0:T(8,128)(2,1)} %fusion.12), kind=kOutput, calls=%fused_computation.135 | convolution fusion | flops 47244640256 | bytes 77594624 | tf_op jit(solution)/shard_map/dot_general | solution.py:76
  715.0 39.4 %multiply_convert_fusion = bf16[8,4,8,256,256]{3,4,2,1,0:T(8,128)(2,1)} fusion(f32[8,4,256,256,8]{3,2,4,1,0:T(8,128)} %get-tuple-element.73, f32[8,4,8,256]{3,2,1,0:T(8,128)S(1)} %copy-done.22, f32[8,4,8,256]{3,2,1,0:T(8,128)S(1)} %copy-done.10, bf16[8,256,4,8,64]{1,4,3,2,0:T(8,128)(2,1)} %get-tuple-element.77, ...), kind=kOutput, calls=%fused_computation.10 | convolution fusion | flops 2248146944 | bytes 110624768 | tf_op jit(solution)/shard_map/while/body/eval_jaxpr/bkgqd,bpkd->bkgqp/dot_general | solution.py:87
  804.1 24.4 %convolution_bitcast_fusion.1 = f32[2048,32,64]{0,2,1:T(8,128)} fusion(bf16[2048,32,64]{0,2,1:T(8,128)(2,1)} %reshape.99, bf16[2048,2048,1]{1,0,2:T(8,128)(2,1)} %bitcast.315), kind=kOutput, calls=%fused_computation.76 | convolution fusion | flops 17179869184 | bytes 33554432 | tf_op jit(solution)/shard_map/nd,nhe->dhe/dot_general | solution.py:108
  862.7 26.7 %bitcast_add_fusion.6 = bf16[8,256,4,64]{1,3,2,0:T(8,128)(2,1)S(1)} fusion(f32[8,256,4,64]{1,3,2,0:T(8,128)} %collective-permute-done.4, f32[8,4,256,256,8]{3,2,4,1,0:T(8,128)} %get-tuple-element.73, f32[8,4,8,256]{3,2,1,0:T(8,128)S(1)} %copy-done.10, bf16[8,256,4,8,64]{1,4,3,2,0:T(8,128)(2,1)} %get-tuple-element.77), kind=kOutput, calls=%fused_computation.88 | convolution fusion | flops 2198863872 | bytes 78905344 | tf_op jit(solution)/shard_map/while/body/eval_jaxpr/bkgqp,bkgqd->bpkd/dot_general | solution.py:86
  889.5 24.6 %convolution_bitcast_fusion = f32[32,64,2048]{2,1,0:T(8,128)} fusion(bf16[32,64,8,256]{3,1,0,2:T(8,128)(2,1)} %bitcast.300, bf16[8,256,2048,1]{2,1,3,0:T(8,128)(2,1)} %bitcast.298), kind=kOutput, calls=%fused_computation.75 | convolution fusion | flops 17179869184 | bytes 33554432 | tf_op jit(solution)/shard_map/bkgqd,bqe->kgde/dot_general | solution.py:79
  929.6 24.6 %fusion.108 = f32[2048,2048,1]{1,0,2:T(8,128)} fusion(bf16[2048,32,64]{0,2,1:T(8,128)(2,1)} %reshape.99, bf16[2048,32,64]{0,2,1:T(8,128)(2,1)} %param.10), kind=kOutput, calls=%fused_computation.133 | convolution fusion | flops 17179869184 | bytes 33554432 | tf_op jit(solution)/shard_map/nhe,dhe->nd/dot_general | solution.py:112
  982.3 257.3 %all-reduce.4.cloned.1.call-done = f32[5632,2048]{1,0:T(8,128)} async-done(((f32[5632,2048]{1,0:T(8,128)}), f32[5632,2048]{1,0:T(8,128)}) %all-reduce.4.cloned.1.call-update) | async-done | bytes 46137360 | tf_op jit(solution)/shard_map/psum | solution.py:116
  1239.6 33.6 %broadcast_multiply_fusion = f32[5632,2048]{1,0:T(8,128)} fusion(f32[5632,2048]{1,0:T(8,128)} %all-reduce.4.cloned.1.call-done), kind=kLoop, calls=%fused_computation.42 | loop fusion | flops 11534336 | bytes 92274688 | tf_op jit(solution)/shard_map/div | solution.py:117
  1273.2 901.2 %all-reduce.6.cloned.1.call-done = (f32[2048,32,64]{0,2,1:T(8,128)}, f32[2048,4,64]{0,2,1:T(8,128)}, f32[2048,4,64]{0,2,1:T(8,128)}, f32[32,64,2048]{2,1,0:T(8,128)}, f32[2048,5632]{1,0:T(8,128)}) async-done(((f32[2048,32,64]{0,2,1:T(8,128)}, f32[2048,4,64]{0,2,1:T(8,128)}, f32[2048,4,64]{0,2,1:T(8,128)}, f32[32,64,2048]{2,1,0:T(8,128)}, f32[2048,5632]{1,0:T(8,128)}), (f32[2048,32,64]{0,2,1:T(8,128)}, ...) | async-done | bytes 83886096 | tf_op jit(solution)/shard_map/psum | solution.py:116
  2199.9 33.5 %broadcast_multiply_fusion.1 = f32[2048,5632]{1,0:T(8,128)} fusion(f32[2048,5632]{1,0:T(8,128)} %get-tuple-element.52), kind=kLoop, calls=%fused_computation.43 | loop fusion | flops 11534336 | bytes 92274688 | tf_op jit(solution)/shard_map/div | solution.py:117
  (106 shorter events, 221.9 us)
Async XLA Ops:
  7.2 1232.4 %all-reduce.4.cloned.1.call-start = ((), (), s32[]{:S(2)}) async-start(), calls=%async_computation | async-start | bytes 92274688 | tf_op jit(solution)/shard_map/psum | solution.py:116
  14.6 171.0 %collective-permute-start.1 = (bf16[8,256,4,64]{1,3,2,0:T(8,128)(2,1)}, bf16[8,256,4,64]{1,3,2,0:T(8,128)(2,1)}, u32[]{:S(2)}, u32[]{:S(2)}) collective-permute-start(bf16[8,256,4,64]{1,3,2,0:T(8,128)(2,1)} %bitcast.280), channel_id=1, source_target_pairs={{0,1},{1,0},{2,3},{3,2},{4,5},{5,4},{6,7},{7,6}} | collective-permute-start | bytes 3145736 | tf_op jit(solution)/shard_map/while/body/eval_jaxpr/ppermute | solution.py:17
  19.1 94.7 %collective-permute-start = (bf16[8,256,4,64]{1,3,2,0:T(8,128)(2,1)}, bf16[8,256,4,64]{1,3,2,0:T(8,128)(2,1)S(1)}, u32[]{:S(2)}, u32[]{:S(2)}) collective-permute-start(bf16[8,256,4,64]{1,3,2,0:T(8,128)(2,1)} %bitcast.281), channel_id=1, source_target_pairs={{0,1},{1,0},{2,3},{3,2},{4,5},{5,4},{6,7},{7,6}} | collective-permute-start | bytes 3145736 | tf_op jit(solution)/shard_map/while/body/eval_jaxpr/ppermute | solution.py:17
  19.5 63.8 %copy-start.8 = (bf16[32,8,8,256]{3,2,1,0:T(8,128)(2,1)}, bf16[32,8,8,256]{3,2,1,0:T(8,128)(2,1)S(1)}, u32[]{:S(2)}) copy-start(bf16[32,8,8,256]{3,2,1,0:T(8,128)(2,1)S(1)} %copy.119) | copy-start | bytes 3145732
  19.8 34.8 %copy-start.3 = (bf16[32,8,8,256]{3,2,1,0:T(8,128)(2,1)}, bf16[32,8,8,256]{3,2,1,0:T(8,128)(2,1)S(1)}, u32[]{:S(2)}) copy-start(bf16[32,8,8,256]{3,2,1,0:T(8,128)(2,1)S(1)} %copy.117) | copy-start | bytes 3145732
  83.2 101.6 %copy-start.1 = (f32[8,4,8,256]{3,2,1,0:T(8,128)}, f32[8,4,8,256]{3,2,1,0:T(8,128)S(1)}, u32[]{:S(2)}) copy-start(f32[8,4,8,256]{3,2,1,0:T(8,128)S(1)} %get-tuple-element.70) | copy-start | bytes 786436
  113.8 28.5 %copy-start.6 = (bf16[8,256,4,64]{1,3,2,0:T(8,128)(2,1)}, bf16[8,256,4,64]{1,3,2,0:T(8,128)(2,1)S(1)}, u32[]{:S(2)}) copy-start(bf16[8,256,4,64]{1,3,2,0:T(8,128)(2,1)S(1)} %collective-permute-done) | copy-start | bytes 3145732
  519.4 26.5 %copy-start.5 = (bf16[2048,2048]{1,0:T(8,128)(2,1)}, bf16[2048,2048]{1,0:T(8,128)(2,1)S(1)}, u32[]{:S(2)}) copy-start(bf16[2048,2048]{1,0:T(8,128)(2,1)S(1)} %add_convert_fusion.1) | copy-start | bytes 25165828
  519.4 26.5 %copy-start.10 = (f32[8,4,8,256]{3,2,1,0:T(8,128)S(1)}, f32[8,4,8,256]{3,2,1,0:T(8,128)}, u32[]{:S(2)}) copy-start(f32[8,4,8,256]{3,2,1,0:T(8,128)} %get-tuple-element.55) | copy-start | bytes 786436
  545.9 27.3 %copy-start.9 = (bf16[32,8,8,256]{3,2,1,0:T(8,128)(2,1)S(1)}, bf16[32,8,8,256]{3,2,1,0:T(8,128)(2,1)}, u32[]{:S(2)}) copy-start(bf16[32,8,8,256]{3,2,1,0:T(8,128)(2,1)} %copy-done.8) | copy-start | bytes 3145732
  545.9 27.3 %copy-start.22 = (f32[8,4,8,256]{3,2,1,0:T(8,128)S(1)}, f32[8,4,8,256]{3,2,1,0:T(8,128)}, u32[]{:S(2)}) copy-start(f32[8,4,8,256]{3,2,1,0:T(8,128)} %get-tuple-element.76) | copy-start | bytes 786436
  613.4 19.3 copy-start.4
  714.4 40.0 %copy-start.7 = (bf16[8,256,4,64]{1,3,2,0:T(8,128)(2,1)S(1)}, bf16[8,256,4,64]{1,3,2,0:T(8,128)(2,1)}, u32[]{:S(2)}) copy-start(bf16[8,256,4,64]{1,3,2,0:T(8,128)(2,1)} %copy-done.6) | copy-start | bytes 3145732
  714.4 1460.0 %all-reduce.6.cloned.1.call-start = ((), (), s32[]{:S(2)}) async-start(), calls=%async_computation.1 | async-start | bytes 167772160 | tf_op jit(solution)/shard_map/psum | solution.py:116
  714.4 129.5 %collective-permute-start.2 = (f32[8,256,4,64]{1,3,2,0:T(8,128)}, f32[8,256,4,64]{1,3,2,0:T(8,128)}, u32[]{:S(2)}, u32[]{:S(2)}) collective-permute-start(f32[8,256,4,64]{1,3,2,0:T(8,128)} %fusion.75), channel_id=1, source_target_pairs={{0,1},{1,0},{2,3},{3,2},{4,5},{5,4},{6,7},{7,6}} | collective-permute-start | bytes 6291464 | tf_op jit(solution)/shard_map/while/body/eval_jaxpr/ppermute | solution.py:17
  714.9 147.8 %collective-permute-start.4 = (f32[8,256,4,64]{1,3,2,0:T(8,128)}, f32[8,256,4,64]{1,3,2,0:T(8,128)}, u32[]{:S(2)}, u32[]{:S(2)}) collective-permute-start(f32[8,256,4,64]{1,3,2,0:T(8,128)} %fusion.66), channel_id=1, source_target_pairs={{0,1},{1,0},{2,3},{3,2},{4,5},{5,4},{6,7},{7,6}} | collective-permute-start | bytes 6291464 | tf_op jit(solution)/shard_map/while/body/eval_jaxpr/ppermute | solution.py:17
  775.1 28.8 %copy-start.2 = (f32[8,4,8,256]{3,2,1,0:T(8,128)S(1)}, f32[8,4,8,256]{3,2,1,0:T(8,128)}, u32[]{:S(2)}) copy-start(f32[8,4,8,256]{3,2,1,0:T(8,128)} %copy-done.1) | copy-start | bytes 786436
  775.1 28.8 %copy-start.12 = (f32[8,4,8,256]{3,2,1,0:T(8,128)S(1)}, f32[8,4,8,256]{3,2,1,0:T(8,128)}, u32[]{:S(2)}) copy-start(f32[8,4,8,256]{3,2,1,0:T(8,128)} %copy-done.11) | copy-start | bytes 786436
  775.1 28.8 %copy-start.14 = (f32[8,4,8,256]{3,2,1,0:T(8,128)S(1)}, f32[8,4,8,256]{3,2,1,0:T(8,128)}, u32[]{:S(2)}) copy-start(f32[8,4,8,256]{3,2,1,0:T(8,128)} %copy-done.13) | copy-start | bytes 786436
  775.1 28.8 %copy-start.16 = (f32[8,4,8,256]{3,2,1,0:T(8,128)S(1)}, f32[8,4,8,256]{3,2,1,0:T(8,128)}, u32[]{:S(2)}) copy-start(f32[8,4,8,256]{3,2,1,0:T(8,128)} %copy-done.15) | copy-start | bytes 786436
  862.2 59.9 %collective-permute-start.3 = (bf16[8,256,4,64]{1,3,2,0:T(8,128)(2,1)}, bf16[8,256,4,64]{1,3,2,0:T(8,128)(2,1)}, u32[]{:S(2)}, u32[]{:S(2)}) collective-permute-start(bf16[8,256,4,64]{1,3,2,0:T(8,128)(2,1)} %bitcast_add_fusion.7), channel_id=1, source_target_pairs={{0,1},{1,0},{2,3},{3,2},{4,5},{5,4},{6,7},{7,6}} | collective-permute-start | bytes 3145736 | tf_op jit(solution)/shard_map/ppermute | solution.py:17
  889.4 24.6 %collective-permute-start.5 = (bf16[8,256,4,64]{1,3,2,0:T(8,128)(2,1)S(1)}, bf16[8,256,4,64]{1,3,2,0:T(8,128)(2,1)S(1)}, u32[]{:S(2)}, u32[]{:S(2)}) collective-permute-start(bf16[8,256,4,64]{1,3,2,0:T(8,128)(2,1)S(1)} %bitcast_add_fusion.6), channel_id=1, source_target_pairs={{0,1},{1,0},{2,3},{3,2},{4,5},{5,4},{6,7},{7,6}} | collective-permute-start | bytes 3145736 | tf_op jit(solution)/shard_map/ppermute | solution.py:17
  929.6 26.1 %copy-start.21 = (bf16[8,256,4,64]{1,3,2,0:T(8,128)(2,1)S(1)}, bf16[8,256,4,64]{1,3,2,0:T(8,128)(2,1)}, u32[]{:S(2)}) copy-start(bf16[8,256,4,64]{1,3,2,0:T(8,128)(2,1)} %copy-done.20) | copy-start | bytes 3145732
  2174.4 19.3 slice-start.3
  (13 other events, 119.3 us)
Sparse Core Ops, SparseCore 0:
  714.5 525.0 all-reduce.3
  1244.8 929.5 all-reduce.5
where the time goes:
time: 2250 us; the launch traced here: 2240 us
  waiting for transfers between devices  1160 us (52%)
  matrix products  865 us (38%)
  other arithmetic  153 us (7%)
  local copies, waits for them, and re-layouts  47.8 us (2%)
    psum x2, waiting for transfers between devices, device_backward(): summed = lax.psum((dw_q, dw_k, dw_v, dw_o, dw_up, dw_down), ('dp', 'cp'))  1160 us
    dot_general x1, matrix products, device_backward(): lax.dot_general(dout_rows, w_down, LAST_CONTRACT, preferred_element_type=...  92.1 us
    div x6, other arithmetic, device_backward(): return (d_x,) + tuple((part_sum / grad_divisor for part_sum in summed))  90.1 us
    dot_general x2, matrix products, backward_block(): jnp.einsum('bkgqd,bpkd->bkgqp', d_attn, v_block, preferred_element_type=j...  79.6 us
    dot_general x2, matrix products, forward_block(): jnp.einsum('bkgqp,bpkd->bkgqd', block_weights.astype(jnp.bfloat16), v_blo...  67.8 us
    dot_general x1, matrix products, device_backward(): lax.dot_general(d_up, w_up, LAST_CONTRACT, preferred_element_type=jnp.flo...  61.4 us
    dot_general x1, matrix products, device_backward(): lax.dot_general(gated, dout_rows, ROW_CONTRACT, preferred_element_type=jn...  60.3 us
    dot_general x1, matrix products, device_backward(): lax.dot_general(hidden_rows, d_up, ROW_CONTRACT, preferred_element_type=j...  59.7 us
  transfers between devices with their start and end apart: 8, of which 2 were waited for; matrix products, arithmetic and copies ran while one was open for 21% of the time, Pallas kernels for 0%

commit v1 on v0

v1 whole, which is shorter than its diff:
```python
import functools
import jax
import jax.numpy as jnp
from jax import lax
from jax.experimental import pallas as pl
from jax.sharding import PartitionSpec as P


F32, BF16 = jnp.float32, jnp.bfloat16
LOG2E = 1.4426950408889634


def dot(a, b, ca, cb):
    return lax.dot_general(a, b, (((ca,), (cb,)), ((), ())), preferred_element_type=F32)


def join_keys(own_ref, other_ref, lo, width):
    return jnp.concatenate([own_ref[:, lo:lo + width], other_ref[:, lo:lo + width]], axis=0)


def attn_fwd_kernel(group, head_dim, q_ref, k_own, k_oth, v_own, v_oth, out_ref, lse_ref):
    coef = head_dim ** -0.5 * LOG2E
    for kv in range(2):
        keys = join_keys(k_own, k_oth, kv * head_dim, head_dim)
        vals = join_keys(v_own, v_oth, kv * head_dim, head_dim)
        outs = []
        for g in range(group):
            head = kv * group + g
            q = q_ref[:, head * head_dim:(head + 1) * head_dim]
            scores = dot(keys, q, 1, 1)
            top = jnp.max(scores, axis=0, keepdims=True)
            probs = jnp.exp2((scores - top) * coef)
            total = jnp.sum(probs, axis=0, keepdims=True)
            out_t = dot(vals, probs.astype(BF16), 0, 0)
            outs.append(out_t * (1.0 / total))
            lse_ref[0, head:head + 1, :] = top * coef + jnp.log(total) * LOG2E
        width = group * head_dim
        out_ref[:, kv * width:(kv + 1) * width] = jnp.concatenate(outs, axis=0).T.astype(BF16)


def attn_bwd_kernel(group, head_dim, q_ref, k_own, k_oth, v_own, v_oth, do_ref, lse_ref, dq_ref, dk_own, dk_oth, dv_own, dv_oth):
    scale = head_dim ** -0.5
    coef = scale * LOG2E
    seq = q_ref.shape[0]
    for kv in range(2):
        keys = join_keys(k_own, k_oth, kv * head_dim, head_dim)
        vals = join_keys(v_own, v_oth, kv * head_dim, head_dim)
        dk = dv = None
        dqs = []
        for g in range(group):
            head = kv * group + g
            cols = slice(head * head_dim, (head + 1) * head_dim)
            q = q_ref[:, cols]
            d_out = do_ref[:, cols]
            probs = jnp.exp2(dot(keys, q, 1, 1) * coef - lse_ref[0, head:head + 1, :])
            d_probs = dot(vals, d_out, 1, 1)
            weighted = probs * d_probs
            delta = jnp.sum(weighted, axis=0, keepdims=True)
            d_scores = (weighted - probs * delta).astype(BF16)
            dv_part = dot(probs.astype(BF16), d_out, 1, 0)
            dk_part = dot(d_scores, q, 1, 0)
            dv = dv_part if dv is None else dv + dv_part
            dk = dk_part if dk is None else dk + dk_part
            dqs.append(dot(keys, d_scores, 0, 0))
        width = group * head_dim
        dq_ref[:, kv * width:(kv + 1) * width] = (jnp.concatenate(dqs, axis=0) * scale).T.astype(BF16)
        lanes = slice(kv * head_dim, (kv + 1) * head_dim)
        dk_own[:, lanes] = dk[:seq] * scale
        dk_oth[:, lanes] = dk[seq:] * scale
        dv_own[:, lanes] = dv[:seq]
        dv_oth[:, lanes] = dv[seq:]


def attention_specs(seq, group, head_dim, kv_heads):
    pairs = kv_heads // 2
    q_spec = pl.BlockSpec((seq, 2 * group * head_dim), lambda b, p: (b, p))
    k_spec = pl.BlockSpec((seq, 2 * head_dim), lambda b, p: (b, p))
    v_spec = pl.BlockSpec((seq, 2 * head_dim), lambda b, p: (b, pairs + p))
    lse_spec = pl.BlockSpec((1, 2 * group, seq), lambda b, p: (b, p, 0))
    return q_spec, k_spec, v_spec, lse_spec


def attention_forward(q, kv_own, kv_oth, batch, seq, heads, kv_heads, head_dim):
    group = heads // kv_heads
    q_spec, k_spec, v_spec, lse_spec = attention_specs(seq, group, head_dim, kv_heads)
    return pl.pallas_call(
        functools.partial(attn_fwd_kernel, group, head_dim),
        grid=(batch, kv_heads // 2),
        in_specs=[q_spec, k_spec, k_spec, v_spec, v_spec],
        out_specs=[q_spec, lse_spec],
        out_shape=[jax.ShapeDtypeStruct(q.shape, BF16), jax.ShapeDtypeStruct((batch, heads, seq), F32)],
        cost_estimate=pl.CostEstimate(flops=40_000_000_000, bytes_accessed=25_000_000, transcendentals=33_000_000),
        name="attn_fwd",
    )(q, kv_own, kv_oth, kv_own, kv_oth)


def attention_backward(q, kv_own, kv_oth, d_attn, lse, batch, seq, heads, kv_heads, head_dim):
    group = heads // kv_heads
    q_spec, k_spec, v_spec, lse_spec = attention_specs(seq, group, head_dim, kv_heads)
    kv_grad = jax.ShapeDtypeStruct((batch * seq, kv_heads * head_dim), F32)
    return pl.pallas_call(
        functools.partial(attn_bwd_kernel, group, head_dim),
        grid=(batch, kv_heads // 2),
        in_specs=[q_spec, k_spec, k_spec, v_spec, v_spec, q_spec, lse_spec],
        out_specs=[q_spec, k_spec, k_spec, k_spec, k_spec],
        out_shape=[jax.ShapeDtypeStruct(q.shape, BF16), kv_grad, kv_grad, kv_grad, kv_grad],
        cost_estimate=pl.CostEstimate(flops=100_000_000_000, bytes_accessed=40_000_000, transcendentals=33_000_000),
        name="attn_bwd",
    )(q, kv_own, kv_oth, kv_own, kv_oth, d_attn, lse)


def solution(mesh):
    dp_size, cp_size = mesh.shape['dp'], mesh.shape['cp']
    assert dp_size == 4 and cp_size == 2
    grad_scale = 1.0 / (dp_size * cp_size)
    first_bit = [1, 2]
    swap_cores = [(c, 1 - c) for c in range(2)]
    both = ('dp', 'cp')

    def pairs(bits):
        return [(2 * d + c, 2 * (d ^ bits[c]) + c) for d in range(4) for c in range(2)]

    first_perm, second_perm = pairs(first_bit), pairs(first_bit[::-1])

    def to_other_core(arrays):
        return lax.ppermute(arrays, 'cp', swap_cores)

    def device_backward(x_in, d_out, w_q, w_k, w_v, w_o, w_up, w_down):
        batch, seq, width = x_in.shape
        heads, head_dim = w_q.shape[1], w_q.shape[2]
        kv_heads = w_k.shape[1]
        rows = batch * seq
        dims = (batch, seq, heads, kv_heads, head_dim)
        x = x_in.reshape(rows, width)
        dout = d_out.reshape(rows, width)
        wq_t = w_q.transpose(1, 2, 0).reshape(heads * head_dim, width)
        wk_t = w_k.transpose(1, 2, 0).reshape(kv_heads * head_dim, width)
        wv_t = w_v.transpose(1, 2, 0).reshape(kv_heads * head_dim, width)
        wkv_t = jnp.concatenate([wk_t, wv_t], axis=0)
        wo = w_o.reshape(heads * head_dim, width)

        chip, core = lax.axis_index('dp'), lax.axis_index('cp')

        def block_order(c):
            bit = 1 + c
            return [(chip ^ 3) * 2 + c, (chip ^ bit) * 2 + c, (chip ^ (3 - bit)) * 2 + c, chip * 2 + c]

        own_order, other_order = block_order(core), block_order(1 - core)

        def take(array, order, axis):
            size = array.shape[axis] // (dp_size * cp_size)
            return jnp.concatenate([lax.dynamic_slice_in_dim(array, i * size, size, axis) for i in order], axis=axis)

        def reduce_block(left, axis, left_oth, right, right_oth, right_axis):
            half = left_oth.shape[axis] // 2

            def own_product(part):
                own = take(left, own_order[2 * part:2 * part + 2], axis)
                return dot(own, right, 1 - axis, right_axis)

            def product(part, own):
                oth = lax.slice_in_dim(left_oth, part * half, (part + 1) * half, axis=axis)
                return own + dot(oth, right_oth, 1 - axis, right_axis)

            own0, own1 = own_product(0), own_product(1)
            arrived = lax.ppermute(product(0, own0), both, first_perm)
            kept = product(1, own1)
            size = kept.shape[0] // 2
            arrived2 = lax.ppermute(kept[:size] + arrived[:size], both, second_perm)
            return kept[size:] + arrived[size:] + arrived2

        def gather(block):
            return lax.all_gather(block, both, axis=0, tiled=True) * grad_scale

        kv = dot(x, wkv_t, 1, 1).astype(BF16)
        kv_oth = to_other_core(kv)
        x_oth = to_other_core(x)
        dout_oth = to_other_core(dout)
        q = dot(x, wq_t, 1, 1).astype(BF16)
        attn, lse = attention_forward(q, kv, kv_oth, *dims)
        attn_oth = to_other_core(take(attn, other_order, 1))
        hidden = (x.astype(F32) + dot(attn, wo, 1, 0)).astype(BF16)
        hid_oth = to_other_core(take(hidden, other_order, 1))
        up_t = dot(w_up, hidden, 0, 1)
        gated, gelu_vjp = jax.vjp(functools.partial(jax.nn.gelu, approximate=True), up_t)
        gated = gated.astype(BF16)
        gated_oth = to_other_core(take(gated, other_order, 0))

        dn_block = reduce_block(gated, 0, gated_oth, dout, dout_oth, 0)
        d_gated = dot(w_down, dout, 1, 1).astype(BF16)
        d_up = gelu_vjp(d_gated.astype(F32))[0].astype(BF16)
        dup_oth = to_other_core(d_up)
        up_block = reduce_block(hidden, 1, hid_oth, d_up, dup_oth, 1)
        d_hid = (dout.astype(F32) + dot(d_up, w_up, 0, 1)).astype(BF16)
        dhid_oth = to_other_core(d_hid)
        o_block = reduce_block(attn, 1, attn_oth, d_hid, dhid_oth, 0)
        d_attn = dot(d_hid, wo, 1, 1).astype(BF16)
        d_attn, dn_block = lax.optimization_barrier((d_attn, dn_block))
        dq, dk, dk_send, dv, dv_send = attention_backward(q, kv, kv_oth, d_attn, lse, *dims)
        dq_oth = to_other_core(take(dq, other_order, 1))
        dk_arr = to_other_core(dk_send)
        dv_arr = to_other_core(dv_send)
        d_kv = jnp.concatenate([(dk + dk_arr).astype(BF16), (dv + dv_arr).astype(BF16)], axis=1)
        q_block = reduce_block(dq, 1, dq_oth, x, x_oth, 0)
        dw_kv = lax.psum(dot(d_kv, x, 0, 0), both) * grad_scale
        d_x = d_hid.astype(F32) + dot(dq, wq_t, 1, 0) + dot(d_kv, wkv_t, 1, 0)
        d_x = d_x.astype(BF16).reshape(x_in.shape)

        dw_down, dw_up = gather(dn_block), gather(up_block)
        dw_o, dw_q = gather(o_block), gather(q_block)

        def weight_shape(grad_t, weight):
            return grad_t.reshape(weight.shape[1], weight.shape[2], width).transpose(2, 0, 1)

        kv_rows = kv_heads * head_dim
        return (d_x, weight_shape(dw_q, w_q), weight_shape(dw_kv[:kv_rows], w_k), weight_shape(dw_kv[kv_rows:], w_v), dw_o.reshape(w_o.shape), dw_up, dw_down)

    act_spec = P('dp', 'cp', None)
    return jax.shard_map(device_backward, mesh=mesh, in_specs=(act_spec, act_spec, P(), P(), P(), P(), P(), P()), out_specs=(act_spec, P(), P(), P(), P(), P(), P()), check_vma=False)
```

time: 2250 us -> 1730 us (0.77)
  waiting for transfers between devices: 1160 us -> 682 us
  matrix products: 865 us -> 572 us
  Pallas kernels: 0 us -> 241 us
    psum x2 -> x1, waiting for transfers between devices: 1160 us -> 0.01 us  [device_backward(): dw_kv = lax.psum(dot(d_kv, x, 0, 0), both) * grad_scale]
    ppermute x6 -> x19, waiting for transfers between devices: 0.02 us -> 576 us  [the longest x4 377 us: reduce_block(): arrived = lax.ppermute(product(0, own0), both, first_perm)]
    dot_general x26, matrix products: 836 us -> 572 us  [dot(): lax.dot_general(a, b, (((ca,), (cb,)), ((), ())), preferred_element_type=...]
    pallas_call x0 -> x2, Pallas kernels: none -> 241 us  [the longest x1 127 us: attention_backward(): pl.pallas_call(functools.partial(attn_bwd_kernel, group, head_dim), grid=...]
    all_gather x0 -> x4, waiting for transfers between devices: none -> 106 us  [gather(): return lax.all_gather(block, both, axis=0, tiled=True) * grad_scale]
    mul x0 -> x5, other arithmetic: none -> 95.9 us  [the longest x4 93.3 us: gather(): return lax.all_gather(block, both, axis=0, tiled=True) * grad_scale]
    div x6 -> x0, other arithmetic: 90.1 us -> none  [device_backward(): return (d_x,) + tuple((part_sum / grad_divisor for part_sum in summed))]
    reduce_sum x1 -> x0, other arithmetic: 41.8 us -> none  [forward_block(): row_sum = row_sum * rescale + jnp.sum(block_weights, axis=-1)]
  transfers between devices with their start and end apart: 8 -> 24, of which waited for: 2 -> 11; matrix products, arithmetic and copies ran while one was open for 21% -> 42% of each run, Pallas kernels for 0% -> 14%
where the time goes in v1:
time: 1730 us
  waiting for transfers between devices  682 us (39%)
  matrix products  572 us (33%)
  Pallas kernels  241 us (14%)
  other arithmetic  152 us (9%)
  local copies, waits for them, and re-layouts  48.5 us (3%)
  starting transfers between devices  20.1 us (1%)
    dot_general x26, matrix products, dot(): lax.dot_general(a, b, (((ca,), (cb,)), ((), ())), preferred_element_type=...  572 us
    ppermute x4, waiting for transfers between devices, reduce_block(): arrived = lax.ppermute(product(0, own0), both, first_perm)  377 us
    ppermute x4, waiting for transfers between devices, reduce_block(): arrived2 = lax.ppermute(kept[:size] + arrived[:size], both, second_perm)  173 us
    pallas_call x1, Pallas kernels, attention_backward(): pl.pallas_call(functools.partial(attn_bwd_kernel, group, head_dim), grid=...  127 us
    pallas_call x1, Pallas kernels, attention_forward(): pl.pallas_call(functools.partial(attn_fwd_kernel, group, head_dim), grid=...  114 us
    all_gather x4, waiting for transfers between devices, gather(): return lax.all_gather(block, both, axis=0, tiled=True) * grad_scale  106 us
    mul x4, other arithmetic, gather(): return lax.all_gather(block, both, axis=0, tiled=True) * grad_scale  93.3 us
  transfers between devices with their start and end apart: 24, of which 11 were waited for; matrix products, arithmetic and copies ran while one was open for 42% of the time, Pallas kernels for 14%

profile of v1, /device:TPU:0, one launch (start us, length us, event | category | flops | bytes accessed | tf_op | source)
XLA Modules:
  0.0 1729.8 jit_solution(17617223623778631213)
XLA Ops:
  29.1 23.6 %convolution_convert_fusion.1.q_ref = bf16[2048,2048]{1,0:T(8,128)(2,1)} fusion(bf16[2048,2048]{1,0:T(8,128)(2,1)} %bitcast.74, bf16[2048,2048]{1,0:T(8,128)(2,1)} %bitcast.86), kind=kOutput, calls=%fused_computation.29 | convolution fusion | flops 17184063488 | bytes 25165824 | tf_op jit(solution)/shard_map/dot_general | solution.py:14
  52.8 113.9 %attn_fwd.1 = (bf16[2048,2048]{1,0:T(8,128)(2,1)}, f32[8,32,256]{2,1,0:T(8,128)}) custom-call(bf16[2048,2048]{1,0:T(8,128)(2,1)} %convolution_convert_fusion.1.q_ref, bf16[2048,512]{1,0:T(8,128)(2,1)} %copy-done.17, bf16[2048,512]{1,0:T(8,128)(2,1)} %collective-permute-done.k_oth.v_oth, bf16[2048,512]{1,0:T(8,128)(2,1)} %copy-done.17, ...), custom_call_target="tpu_custom_call" | custom-call | flops 40000000000 | bytes 25000000 | tf_op jit(solution)/shard_map/attn_fwd/pallas_call | solution.py:86
  175.1 23.3 %add_convert_fusion.2 = bf16[2048,2048]{0,1:T(8,128)(2,1)S(1)} fusion(bf16[2048,2048]{0,1:T(8,128)(2,1)} %copy.20, bf16[2048,2048]{1,0:T(8,128)(2,1)} %get-tuple-element.16, bf16[2048,2048]{1,0:T(8,128)(2,1)} %bitcast.84), kind=kOutput, calls=%fused_computation.20 | convolution fusion | flops 17192452096 | bytes 33554432 | tf_op jit(solution)/shard_map/dot_general | solution.py:14
  198.4 70.4 %fusion.10 = (bf16[5632,2048]{1,0:T(8,128)(2,1)}, f32[2048,5632]{0,1:T(8,128)}) fusion(bf16[2048,2048]{0,1:T(8,128)(2,1)S(1)} %add_convert_fusion.2, bf16[2048,5632]{1,0:T(8,128)(2,1)} %param.14), kind=kOutput, calls=%fused_computation.15 | convolution fusion | flops 47348449280 | bytes 100663296 | tf_op jit(solution)/shard_map/dot_general | solution.py:14
  311.2 80.6 %fusion.2 = bf16[5632,2048]{1,0:T(8,128)(2,1)} fusion(f32[2048,5632]{0,1:T(8,128)} %get-tuple-element.60, bf16[5632,2048]{1,0:T(8,128)(2,1)} %param.15, bf16[2048,2048]{1,0:T(8,128)(2,1)} %bitcast), kind=kOutput, calls=%fused_computation.6 | convolution fusion | flops 47498395648 | bytes 100663296 | tf_op jit(solution)/shard_map/dot_general | solution.py:14
  391.7 20.8 %convolution_add_fusion.2 = f32[1408,2048]{1,0:T(8,128)} fusion(f32[1408,2048]{1,0:T(8,128)} %fusion.19, bf16[2048,2048]{1,0:T(8,128)(2,1)} %collective-permute-done.2, bf16[2816,2048]{1,0:T(8,128)(2,1)} %collective-permute-done.1), kind=kOutput, calls=%fused_computation.24 | convolution fusion | flops 11814043648 | bytes 37224448 | tf_op jit(solution)/shard_map/dot_general | solution.py:14
  415.5 66.1 %add_convert_fusion.1 = bf16[2048,2048]{1,0:T(8,128)(2,1)} fusion(bf16[2048,2048]{1,0:T(8,128)(2,1)} %bitcast, bf16[5632,2048]{1,0:T(8,128)(2,1)} %fusion.2, bf16[2048,5632]{1,0:T(8,128)(2,1)} %param.14), kind=kOutput, calls=%fused_computation.19 | convolution fusion | flops 47257223168 | bytes 62914560 | tf_op jit(solution)/shard_map/dot_general | solution.py:14
  504.7 20.7 %convolution_add_fusion.3 = f32[1408,2048]{1,0:T(8,128)} fusion(f32[1408,2048]{1,0:T(8,128)} %fusion.15, bf16[2048,2048]{1,0:T(8,128)(2,1)} %collective-permute-done.2, bf16[2816,2048]{1,0:T(8,128)(2,1)} %collective-permute-done.1), kind=kOutput, calls=%fused_computation.25 | convolution fusion | flops 11814043648 | bytes 37224448 | tf_op jit(solution)/shard_map/dot_general | solution.py:14
  558.1 24.1 %convolution_convert_fusion.do_ref = bf16[2048,2048]{1,0:T(8,128)(2,1)} fusion(bf16[2048,2048]{1,0:T(8,128)(2,1)} %add_convert_fusion.1, bf16[2048,2048]{1,0:T(8,128)(2,1)} %bitcast.85), kind=kOutput, calls=%fused_computation.28 | convolution fusion | flops 17184063488 | bytes 25165824 | tf_op jit(solution)/shard_map/dot_general | solution.py:14
  593.0 37.7 %collective-permute-done.4 = f32[704,2048]{1,0:T(8,128)} collective-permute-done((f32[704,2048]{1,0:T(8,128)S(1)}, f32[704,2048]{1,0:T(8,128)}, u32[]{:S(2)}, u32[]{:S(2)}) %collective-permute-start.4) | collective-permute-done | bytes 5767200 | tf_op jit(solution)/shard_map/ppermute | solution.py:169
  641.7 126.8 %attn_bwd.1 = (bf16[2048,2048]{1,0:T(8,128)(2,1)}, f32[2048,256]{1,0:T(8,128)}, f32[2048,256]{1,0:T(8,128)}, f32[2048,256]{1,0:T(8,128)}, f32[2048,256]{1,0:T(8,128)}) custom-call(bf16[2048,2048]{1,0:T(8,128)(2,1)} %convolution_convert_fusion.1.q_ref, bf16[2048,512]{1,0:T(8,128)(2,1)} %copy-done.17, bf16[2048,512]{1,0:T(8,128)(2,1)} %collective-permute-done.k_oth.v_oth, ...), custom_call_target="tpu_custom_call" | custom-call | flops 99999997952 | bytes 40000000 | tf_op jit(solution)/shard_map/attn_bwd/pallas_call | solution.py:101
  794.5 31.5 %collective-permute-done.14 = f32[256,2048]{1,0:T(8,128)} collective-permute-done((f32[256,2048]{1,0:T(8,128)S(1)}, f32[256,2048]{1,0:T(8,128)}, u32[]{:S(2)}, u32[]{:S(2)}) %collective-permute-start.14) | collective-permute-done | bytes 2097184 | tf_op jit(solution)/shard_map/ppermute | solution.py:169
  880.9 85.8 %collective-permute-done.9 = f32[512,2048]{1,0:T(8,128)S(1)} collective-permute-done((f32[512,2048]{1,0:T(8,128)S(1)}, f32[512,2048]{1,0:T(8,128)S(1)}, u32[]{:S(2)}, u32[]{:S(2)}) %collective-permute-start.9) | collective-permute-done | bytes 4194336 | tf_op jit(solution)/shard_map/ppermute | solution.py:166
  968.5 40.1 %collective-permute-done.10 = f32[256,2048]{1,0:T(8,128)S(1)} collective-permute-done((f32[256,2048]{1,0:T(8,128)S(1)}, f32[256,2048]{1,0:T(8,128)S(1)}, u32[]{:S(2)}, u32[]{:S(2)}) %collective-permute-start.10) | collective-permute-done | bytes 2097184 | tf_op jit(solution)/shard_map/ppermute | solution.py:169
  1019.7 19.4 %fusion.52 = f32[512,5632]{1,0:T(8,128)} fusion(bf16[5632,2048]{1,0:T(8,128)(2,1)} %fusion.2, bf16[2048,256]{0,1:T(8,128)(2,1)S(1)} %get-tuple-element.34, bf16[2048,256]{0,1:T(8,128)(2,1)} %get-tuple-element.35), kind=kOutput, calls=%fused_computation.89 | convolution fusion | flops 11815354368 | bytes 36700160 | tf_op jit(solution)/shard_map/dot_general | solution.py:14
  1057.6 22.6 %convolution_add_fusion = f32[512,5632]{1,0:T(8,128)} fusion(f32[512,5632]{1,0:T(8,128)} %fusion.52, bf16[5632,2048]{1,0:T(8,128)(2,1)} %collective-permute-done.16, bf16[2048,1024]{0,1:T(8,128)(2,1)} %collective-permute-done.15), kind=kOutput, calls=%fused_computation.22 | convolution fusion | flops 11814043648 | bytes 48234496 | tf_op jit(solution)/shard_map/dot_general | solution.py:14
  1081.4 19.6 %fusion.48 = f32[512,5632]{1,0:T(8,128)} fusion(bf16[5632,2048]{1,0:T(8,128)(2,1)} %fusion.2, bf16[2048,256]{0,1:T(8,128)(2,1)S(1)} %get-tuple-element.40, bf16[2048,256]{0,1:T(8,128)(2,1)S(1)} %get-tuple-element.33), kind=kOutput, calls=%fused_computation.85 | convolution fusion | flops 11815354368 | bytes 36700160 | tf_op jit(solution)/shard_map/dot_general | solution.py:14
  1101.0 24.6 %convolution_add_fusion.1 = f32[512,5632]{1,0:T(8,128)} fusion(f32[512,5632]{1,0:T(8,128)} %fusion.48, bf16[5632,2048]{1,0:T(8,128)(2,1)} %collective-permute-done.16, bf16[2048,1024]{0,1:T(8,128)(2,1)} %collective-permute-done.15), kind=kOutput, calls=%fused_computation.23 | convolution fusion | flops 11814043648 | bytes 48234496 | tf_op jit(solution)/shard_map/dot_general | solution.py:14
  1125.6 275.8 %collective-permute-done.17 = f32[512,5632]{1,0:T(8,128)} collective-permute-done((f32[512,5632]{1,0:T(8,128)}, f32[512,5632]{1,0:T(8,128)}, u32[]{:S(2)}, u32[]{:S(2)}) %collective-permute-start.17) | collective-permute-done | bytes 11534368 | tf_op jit(solution)/shard_map/ppermute | solution.py:166
  1407.9 63.9 %collective-permute-done.18 = f32[256,5632]{1,0:T(8,128)S(1)} collective-permute-done((f32[256,5632]{1,0:T(8,128)S(1)}, f32[256,5632]{1,0:T(8,128)S(1)}, u32[]{:S(2)}, u32[]{:S(2)}) %collective-permute-start.18) | collective-permute-done | bytes 5767200 | tf_op jit(solution)/shard_map/ppermute | solution.py:169
  1480.4 25.3 %fusion.70 = f32[2048,2048]{1,0:T(8,128)} fusion(bf16[2048,2048]{1,0:T(8,128)(2,1)} %get-tuple-element.19, bf16[2048,2048]{1,0:T(8,128)(2,1)} %bitcast.87), kind=kOutput, calls=%fused_computation.142 | convolution fusion | flops 17179869184 | bytes 33554432 | tf_op jit(solution)/shard_map/dot_general | solution.py:14
  1547.9 35.9 %broadcast_multiply_fusion = f32[5632,2048]{1,0:T(8,128)} fusion(f32[5632,2048]{1,0:T(8,128)} %all-gather.11.cloned.1.call-done), kind=kLoop, calls=%fused_computation.16 | loop fusion | flops 11534336 | bytes 92274688 | tf_op jit(solution)/shard_map/mul | solution.py:173
  1583.8 105.7 %all-gather.9.cloned.1.call-done = f32[2048,5632]{1,0:T(8,128)} async-done(((f32[256,5632]{1,0:T(8,128)}), f32[2048,5632]{1,0:T(8,128)}) %all-gather.9.cloned.1.call-update) | async-done | bytes 46137360 | tf_op jit(solution)/shard_map/all_gather | solution.py:173
  1689.5 33.5 %broadcast_multiply_fusion.1 = f32[2048,5632]{1,0:T(8,128)} fusion(f32[2048,5632]{1,0:T(8,128)} %all-gather.9.cloned.1.call-done), kind=kLoop, calls=%fused_computation.17 | loop fusion | flops 11534336 | bytes 92274688 | tf_op jit(solution)/shard_map/mul | solution.py:173
  (130 shorter events, 324.0 us)
Async XLA Ops:
  7.2 1512.0 %all-reduce.2.cloned.1.call-start = ((), (), s32[]{:S(2)}) async-start(), calls=%async_computation.1 | async-start | bytes 8388608 | tf_op jit(solution)/shard_map/psum | solution.py:205
  15.8 36.9 %collective-permute-start = (bf16[2048,512]{1,0:T(8,128)(2,1)S(1)}, bf16[2048,512]{1,0:T(8,128)(2,1)}, u32[]{:S(2)}, u32[]{:S(2)}) collective-permute-start(bf16[2048,512]{1,0:T(8,128)(2,1)S(1)} %fusion.23.k_own.v_own), channel_id=1, source_target_pairs={{0,1},{1,0},{2,3},{3,2},{4,5},{5,4},{6,7},{7,6}} | collective-permute-start | bytes 6291464 | tf_op jit(solution)/shard_map/ppermute | solution.py:126
  16.7 375.0 %collective-permute-start.2 = (bf16[2048,2048]{1,0:T(8,128)(2,1)}, bf16[2048,2048]{1,0:T(8,128)(2,1)}, u32[]{:S(2)}, u32[]{:S(2)}) collective-permute-start(bf16[2048,2048]{1,0:T(8,128)(2,1)} %bitcast), channel_id=1, source_target_pairs={{0,1},{1,0},{2,3},{3,2},{4,5},{5,4},{6,7},{7,6}} | collective-permute-start | bytes 25165832 | tf_op jit(solution)/shard_map/ppermute | solution.py:126
  174.6 407.6 %collective-permute-start.11 = (bf16[2048,1024]{1,0:T(8,128)(2,1)}, bf16[2048,1024]{1,0:T(8,128)(2,1)}, u32[]{:S(2)}, u32[]{:S(2)}) collective-permute-start(bf16[2048,1024]{1,0:T(8,128)(2,1)} %pad_maximum_fusion.2), channel_id=1, source_target_pairs={{0,1},{1,0},{2,3},{3,2},{4,5},{5,4},{6,7},{7,6}} | collective-permute-start | bytes 12582920 | tf_op jit(solution)/shard_map/ppermute | solution.py:126
  293.7 98.0 %collective-permute-start.1 = (bf16[2816,2048]{1,0:T(8,128)(2,1)}, bf16[2816,2048]{1,0:T(8,128)(2,1)}, u32[]{:S(2)}, u32[]{:S(2)}) collective-permute-start(bf16[2816,2048]{1,0:T(8,128)(2,1)} %pad_maximum_fusion), channel_id=1, source_target_pairs={{0,1},{1,0},{2,3},{3,2},{4,5},{5,4},{6,7},{7,6}} | collective-permute-start | bytes 34603016 | tf_op jit(solution)/shard_map/ppermute | solution.py:126
  412.6 128.4 %collective-permute-start.3 = (f32[1408,2048]{1,0:T(8,128)}, f32[1408,2048]{1,0:T(8,128)}, u32[]{:S(2)}, u32[]{:S(2)}) collective-permute-start(f32[1408,2048]{1,0:T(8,128)} %convolution_add_fusion.2), channel_id=1, source_target_pairs={{0,2},{1,5},{2,0},{3,7},{4,6},{5,1},{6,4},{7,3}} | collective-permute-start | bytes 34603016 | tf_op jit(solution)/shard_map/ppermute | solution.py:166
  481.5 100.7 %collective-permute-start.12 = (bf16[2048,2048]{1,0:T(8,128)(2,1)}, bf16[2048,2048]{1,0:T(8,128)(2,1)S(1)}, u32[]{:S(2)}, u32[]{:S(2)}) collective-permute-start(bf16[2048,2048]{1,0:T(8,128)(2,1)} %add_convert_fusion.1), channel_id=1, source_target_pairs={{0,1},{1,0},{2,3},{3,2},{4,5},{5,4},{6,7},{7,6}} | collective-permute-start | bytes 25165832 | tf_op jit(solution)/shard_map/ppermute | solution.py:126
  546.4 84.2 %collective-permute-start.4 = (f32[704,2048]{1,0:T(8,128)S(1)}, f32[704,2048]{1,0:T(8,128)}, u32[]{:S(2)}, u32[]{:S(2)}) collective-permute-start(f32[704,2048]{1,0:T(8,128)S(1)} %slice_add_fusion.2), channel_id=1, source_target_pairs={{0,4},{1,3},{2,6},{3,1},{4,0},{5,7},{6,2},{7,5}} | collective-permute-start | bytes 17301512 | tf_op jit(solution)/shard_map/ppermute | solution.py:169
  591.5 187.7 %collective-permute-start.13 = (f32[512,2048]{1,0:T(8,128)}, f32[512,2048]{1,0:T(8,128)}, u32[]{:S(2)}, u32[]{:S(2)}) collective-permute-start(f32[512,2048]{1,0:T(8,128)} %convolution_add_fusion.4), channel_id=1, source_target_pairs={{0,2},{1,5},{2,0},{3,7},{4,6},{5,1},{6,4},{7,3}} | collective-permute-start | bytes 12582920 | tf_op jit(solution)/shard_map/ppermute | solution.py:166
  768.4 16.7 collective-permute-start.5
  768.5 17.1 collective-permute-start.6
  782.6 43.4 %collective-permute-start.14 = (f32[256,2048]{1,0:T(8,128)S(1)}, f32[256,2048]{1,0:T(8,128)}, u32[]{:S(2)}, u32[]{:S(2)}) collective-permute-start(f32[256,2048]{1,0:T(8,128)S(1)} %slice_add_fusion.4), channel_id=1, source_target_pairs={{0,4},{1,3},{2,6},{3,1},{4,0},{5,7},{6,2},{7,5}} | collective-permute-start | bytes 6291464 | tf_op jit(solution)/shard_map/ppermute | solution.py:169
  794.5 729.5 %all-gather.7.cloned.1.call-start = ((), (), s32[]{:S(2)}) async-start(), calls=%async_computation.2 | async-start | bytes 18874368 | tf_op jit(solution)/shard_map/all_gather | solution.py:173
  831.0 704.9 %all-gather.5.cloned.1.call-start = ((), (), s32[]{:S(2)}) async-start(), calls=%async_computation | async-start | bytes 18874368 | tf_op jit(solution)/shard_map/all_gather | solution.py:173
  831.0 13.5 collective-permute-start.8
  836.3 14.3 collective-permute-start.7
  861.1 105.6 %collective-permute-start.9 = (f32[512,2048]{1,0:T(8,128)S(1)}, f32[512,2048]{1,0:T(8,128)S(1)}, u32[]{:S(2)}, u32[]{:S(2)}) collective-permute-start(f32[512,2048]{1,0:T(8,128)S(1)} %convolution_add_fusion.6), channel_id=1, source_target_pairs={{0,2},{1,5},{2,0},{3,7},{4,6},{5,1},{6,4},{7,3}} | collective-permute-start | bytes 12582920 | tf_op jit(solution)/shard_map/ppermute | solution.py:166
  967.0 41.6 %collective-permute-start.10 = (f32[256,2048]{1,0:T(8,128)S(1)}, f32[256,2048]{1,0:T(8,128)S(1)}, u32[]{:S(2)}, u32[]{:S(2)}) collective-permute-start(f32[256,2048]{1,0:T(8,128)S(1)} %slice_add_fusion.6), channel_id=1, source_target_pairs={{0,4},{1,3},{2,6},{3,1},{4,0},{5,7},{6,2},{7,5}} | collective-permute-start | bytes 6291464 | tf_op jit(solution)/shard_map/ppermute | solution.py:169
  1010.5 537.4 %all-gather.11.cloned.1.call-start = ((), (), s32[]{:S(2)}) async-start(), calls=%async_computation.4 | async-start | bytes 51904512 | tf_op jit(solution)/shard_map/all_gather | solution.py:173
  1011.1 678.4 %all-gather.9.cloned.1.call-start = ((), (), s32[]{:S(2)}) async-start(), calls=%async_computation.3 | async-start | bytes 51904512 | tf_op jit(solution)/shard_map/all_gather | solution.py:173
  1011.1 46.5 %collective-permute-start.16 = (bf16[5632,2048]{1,0:T(8,128)(2,1)}, bf16[5632,2048]{1,0:T(8,128)(2,1)}, u32[]{:S(2)}, u32[]{:S(2)}) collective-permute-start(bf16[5632,2048]{1,0:T(8,128)(2,1)} %fusion.2), channel_id=1, source_target_pairs={{0,1},{1,0},{2,3},{3,2},{4,5},{5,4},{6,7},{7,6}} | collective-permute-start | bytes 69206024 | tf_op jit(solution)/shard_map/ppermute | solution.py:126
  1019.1 38.5 %collective-permute-start.15 = (bf16[2048,1024]{0,1:T(8,128)(2,1)}, bf16[2048,1024]{0,1:T(8,128)(2,1)}, u32[]{:S(2)}, u32[]{:S(2)}) collective-permute-start(bf16[2048,1024]{0,1:T(8,128)(2,1)} %pad_maximum_fusion.3), channel_id=1, source_target_pairs={{0,1},{1,0},{2,3},{3,2},{4,5},{5,4},{6,7},{7,6}} | collective-permute-start | bytes 12582920 | tf_op jit(solution)/shard_map/ppermute | solution.py:126
  1080.2 321.3 %collective-permute-start.17 = (f32[512,5632]{1,0:T(8,128)}, f32[512,5632]{1,0:T(8,128)}, u32[]{:S(2)}, u32[]{:S(2)}) collective-permute-start(f32[512,5632]{1,0:T(8,128)} %convolution_add_fusion), channel_id=1, source_target_pairs={{0,2},{1,5},{2,0},{3,7},{4,6},{5,1},{6,4},{7,3}} | collective-permute-start | bytes 34603016 | tf_op jit(solution)/shard_map/ppermute | solution.py:166
  1406.4 65.4 %collective-permute-start.18 = (f32[256,5632]{1,0:T(8,128)S(1)}, f32[256,5632]{1,0:T(8,128)S(1)}, u32[]{:S(2)}, u32[]{:S(2)}) collective-permute-start(f32[256,5632]{1,0:T(8,128)S(1)} %slice_add_fusion), channel_id=1, source_target_pairs={{0,4},{1,3},{2,6},{3,1},{4,0},{5,7},{6,2},{7,5}} | collective-permute-start | bytes 17301512 | tf_op jit(solution)/shard_map/ppermute | solution.py:169
  (23 other events, 413.3 us)
Sparse Core Ops, SparseCore 0:
  794.6 84.5 all-reduce.1
  881.0 115.3 all-gather.6
  1010.6 88.9 all-gather.4
  1101.3 302.1 all-gather.10
  1480.5 208.9 all-gather.8

commit v2 on v1

--- a/solution.py
+++ b/solution.py
@@ -151,63 +151,99 @@
             size = array.shape[axis] // (dp_size * cp_size)
             return jnp.concatenate([lax.dynamic_slice_in_dim(array, i * size, size, axis) for i in order], axis=axis)
 
-        def reduce_block(left, axis, left_oth, right, right_oth, right_axis):
-            half = left_oth.shape[axis] // 2
-
-            def own_product(part):
-                own = take(left, own_order[2 * part:2 * part + 2], axis)
-                return dot(own, right, 1 - axis, right_axis)
-
-            def product(part, own):
-                oth = lax.slice_in_dim(left_oth, part * half, (part + 1) * half, axis=axis)
-                return own + dot(oth, right_oth, 1 - axis, right_axis)
-
-            own0, own1 = own_product(0), own_product(1)
-            arrived = lax.ppermute(product(0, own0), both, first_perm)
-            kept = product(1, own1)
+        def block_of(array, i, axis):
+            size = array.shape[axis] // (dp_size * cp_size)
+            return lax.dynamic_slice_in_dim(array, i * size, size, axis)
+
+        def own_products(left, right, right_axis):
+            parts = [take(left, own_order[p:p + 2], 1) for p in (0, 2)]
+            return [lax.optimization_barrier(dot(part, right, 0, right_axis)) for part in parts]
+
+        def add_product(part, own, left_oth, right_oth, right_axis):
+            half = left_oth.shape[1] // 2
+            oth = left_oth[:, part * half:(part + 1) * half]
+            return own + dot(oth, right_oth, 0, right_axis)
+
+        def first_exchange(sent, kept):
+            arrived = lax.ppermute(sent, both, first_perm)
             size = kept.shape[0] // 2
-            arrived2 = lax.ppermute(kept[:size] + arrived[:size], both, second_perm)
-            return kept[size:] + arrived[size:] + arrived2
+            return kept[:size] + arrived[:size], (kept[size:], arrived[size:])
+
+        def second_exchange(middle, rest):
+            return rest[0] + rest[1] + lax.ppermute(middle, both, second_perm)
 
         def gather(block):
-            return lax.all_gather(block, both, axis=0, tiled=True) * grad_scale
+            return lax.all_gather(block, both, axis=0, tiled=True)
 
         kv = dot(x, wkv_t, 1, 1).astype(BF16)
         kv_oth = to_other_core(kv)
-        x_oth = to_other_core(x)
         dout_oth = to_other_core(dout)
         q = dot(x, wq_t, 1, 1).astype(BF16)
         attn, lse = attention_forward(q, kv, kv_oth, *dims)
-        attn_oth = to_other_core(take(attn, other_order, 1))
         hidden = (x.astype(F32) + dot(attn, wo, 1, 0)).astype(BF16)
-        hid_oth = to_other_core(take(hidden, other_order, 1))
         up_t = dot(w_up, hidden, 0, 1)
         gated, gelu_vjp = jax.vjp(functools.partial(jax.nn.gelu, approximate=True), up_t)
         gated = gated.astype(BF16)
-        gated_oth = to_other_core(take(gated, other_order, 0))
-
-        dn_block = reduce_block(gated, 0, gated_oth, dout, dout_oth, 0)
+        gated_oths = [to_other_core(block_of(gated, i, 0)) for i in other_order]
+
+        def dn_product(i, own):
+            return own + dot(gated_oths[i], dout_oth, 1, 0)
+
+        dn_own = [lax.optimization_barrier(dot(block_of(gated, i, 0), dout, 1, 0)) for i in own_order]
+        dn_sent = dn_product(0, dn_own[0])
+        arrived_a = lax.ppermute(dn_sent, both, first_perm)
+        arrived_b = lax.ppermute(dn_product(1, dn_own[1]), both, first_perm)
+        dn_middle = dn_product(2, dn_own[2]) + arrived_a
+        dn_block = second_exchange(dn_middle, (dn_product(3, dn_own[3]), arrived_b))
+
         d_gated = dot(w_down, dout, 1, 1).astype(BF16)
         d_up = gelu_vjp(d_gated.astype(F32))[0].astype(BF16)
         dup_oth = to_other_core(d_up)
-        up_block = reduce_block(hidden, 1, hid_oth, d_up, dup_oth, 1)
+        d_up, dn_block, hid_late, attn_late = lax.optimization_barrier((d_up, dn_block, hidden, attn))
+        hid_oth = to_other_core(take(hid_late, other_order, 1))
+        attn_oth = to_other_core(take(attn_late, other_order, 1))
+        up_own = own_products(hid_late, d_up, 1)
+        up_sent = add_product(0, up_own[0], hid_oth, dup_oth, 1)
+        up_kept = add_product(1, up_own[1], hid_oth, dup_oth, 1)
+        up_middle, up_rest = first_exchange(up_sent, up_kept)
+
         d_hid = (dout.astype(F32) + dot(d_up, w_up, 0, 1)).astype(BF16)
         dhid_oth = to_other_core(d_hid)
-        o_block = reduce_block(attn, 1, attn_oth, d_hid, dhid_oth, 0)
         d_attn = dot(d_hid, wo, 1, 1).astype(BF16)
-        d_attn, dn_block = lax.optimization_barrier((d_attn, dn_block))
+        o_own = own_products(attn_late, d_hid, 0)
+        o_sent = add_product(0, o_own[0], attn_oth, dhid_oth, 0)
+        x_late, d_attn, o_sent, up_middle = lax.optimization_barrier((x, d_attn, o_sent, up_middle))
+        o_kept = add_product(1, o_own[1], attn_oth, dhid_oth, 0)
+        o_middle, o_rest = first_exchange(o_sent, o_kept)
+        up_block = second_exchange(up_middle, up_rest)
+        x_oth = to_other_core(x_late)
+
         dq, dk, dk_send, dv, dv_send = attention_backward(q, kv, kv_oth, d_attn, lse, *dims)
+        dq, o_middle, up_block = lax.optimization_barrier((dq, o_middle, up_block))
+        o_block = second_exchange(o_middle, o_rest)
         dq_oth = to_other_core(take(dq, other_order, 1))
         dk_arr = to_other_core(dk_send)
         dv_arr = to_other_core(dv_send)
         d_kv = jnp.concatenate([(dk + dk_arr).astype(BF16), (dv + dv_arr).astype(BF16)], axis=1)
-        q_block = reduce_block(dq, 1, dq_oth, x, x_oth, 0)
-        dw_kv = lax.psum(dot(d_kv, x, 0, 0), both) * grad_scale
+        q_own = own_products(dq, x_late, 0)
+        q_sent = add_product(0, q_own[0], dq_oth, x_oth, 0)
+        q_kept = add_product(1, q_own[1], dq_oth, x_oth, 0)
+        q_block = second_exchange(*first_exchange(q_sent, q_kept))
+        dw_kv = dot(d_kv, x_late, 0, 0)
+        dw_kv = take(dw_kv, own_order, 0) + to_other_core(take(dw_kv, other_order, 0))
+        kv_half = dw_kv.shape[0] // 2
+        kv_block = second_exchange(*first_exchange(dw_kv[:kv_half], dw_kv[kv_half:]))
         d_x = d_hid.astype(F32) + dot(dq, wq_t, 1, 0) + dot(d_kv, wkv_t, 1, 0)
         d_x = d_x.astype(BF16).reshape(x_in.shape)
 
-        dw_down, dw_up = gather(dn_block), gather(up_block)
-        dw_o, dw_q = gather(o_block), gather(q_block)
+        dw_down = gather(dn_block) * grad_scale
+        dw_up = gather(up_block) * grad_scale
+        dw_o = gather(o_block) * grad_scale
+        qkv = gather(jnp.concatenate([q_block, kv_block], axis=0))
+        q_size = q_block.shape[0]
+        qkv = qkv.reshape(dp_size * cp_size, q_size + kv_block.shape[0], width)
+        dw_q = qkv[:, :q_size].reshape(-1, width) * grad_scale
+        dw_kv = qkv[:, q_size:].reshape(-1, width) * grad_scale
 
         def weight_shape(grad_t, weight):
             return grad_t.reshape(weight.shape[1], weight.shape[2], width).transpose(2, 0, 1)

time: 1730 us -> 1660 us (0.960)
  waiting for transfers between devices: 682 us -> 619 us
  local copies, waits for them, and re-layouts: 48.5 us -> 27.5 us
    ppermute x8 -> x11, waiting for transfers between devices: 550 us -> 198 us  [the longest x4 126 us: first_exchange(): arrived = lax.ppermute(sent, both, first_perm)]
    all_gather x4, waiting for transfers between devices: 106 us -> 413 us  [gather(): return lax.all_gather(block, both, axis=0, tiled=True)]
    ppermute x11 -> x15, waiting for transfers between devices: 25.6 us -> 7.21 us  [to_other_core(): return lax.ppermute(arrays, 'cp', swap_cores)]
    add x8 -> x11, other arithmetic: 40.5 us -> 46.1 us  [the longest x5 28 us: second_exchange(): return rest[0] + rest[1] + lax.ppermute(middle, both, second_perm)]
    dot_general x26 -> x30, matrix products: 572 us -> 574 us  [dot(): lax.dot_general(a, b, (((ca,), (cb,)), ((), ())), preferred_element_type=...]
  transfers between devices with their start and end apart: 24 -> 30, of which waited for: 11 -> 12; matrix products, arithmetic and copies ran while one was open for 42% -> 42% of each run, Pallas kernels for 14% -> 15%
where the time goes in v2:
time: 1660 us
  waiting for transfers between devices  619 us (37%)
  matrix products  574 us (35%)
  Pallas kernels  241 us (15%)
  other arithmetic  161 us (10%)
  local copies, waits for them, and re-layouts  27.5 us (2%)
  starting transfers between devices  22.3 us (1%)
    dot_general x30, matrix products, dot(): lax.dot_general(a, b, (((ca,), (cb,)), ((), ())), preferred_element_type=...  574 us
    all_gather x4, waiting for transfers between devices, gather(): return lax.all_gather(block, both, axis=0, tiled=True)  413 us
    pallas_call x1, Pallas kernels, attention_backward(): pl.pallas_call(functools.partial(attn_bwd_kernel, group, head_dim), grid=...  127 us
    ppermute x4, waiting for transfers between devices, first_exchange(): arrived = lax.ppermute(sent, both, first_perm)  126 us
    pallas_call x1, Pallas kernels, attention_forward(): pl.pallas_call(functools.partial(attn_fwd_kernel, group, head_dim), grid=...  114 us
    ppermute x5, waiting for transfers between devices, second_exchange(): return rest[0] + rest[1] + lax.ppermute(middle, both, second_perm)  51.4 us
    mul x1, other arithmetic, device_backward(): dw_down = gather(dn_block) * grad_scale  34.1 us
    mul x1, other arithmetic, device_backward(): dw_up = gather(up_block) * grad_scale  33.5 us
  transfers between devices with their start and end apart: 30, of which 12 were waited for; matrix products, arithmetic and copies ran while one was open for 42% of the time, Pallas kernels for 15%

profile of v2, /device:TPU:0, one launch (start us, length us, event | category | flops | bytes accessed | tf_op | source)
XLA Modules:
  0.0 1659.0 jit_solution(6340159241471575906)
XLA Ops:
  16.7 23.8 %convolution_convert_fusion.1.q_ref = bf16[2048,2048]{1,0:T(8,128)(2,1)} fusion(bf16[2048,2048]{1,0:T(8,128)(2,1)} %bitcast.86, bf16[2048,2048]{1,0:T(8,128)(2,1)} %bitcast.94), kind=kOutput, calls=%fused_computation.26 | convolution fusion | flops 17184063488 | bytes 25165824 | tf_op jit(solution)/shard_map/dot_general | solution.py:14
  40.6 113.9 %attn_fwd.1 = (bf16[2048,2048]{1,0:T(8,128)(2,1)}, f32[8,32,256]{2,1,0:T(8,128)}) custom-call(bf16[2048,2048]{1,0:T(8,128)(2,1)} %convolution_convert_fusion.1.q_ref, bf16[2048,512]{1,0:T(8,128)(2,1)} %copy-done.15, bf16[2048,512]{1,0:T(8,128)(2,1)} %collective-permute-done.k_oth.v_oth, bf16[2048,512]{1,0:T(8,128)(2,1)} %copy-done.15, ...), custom_call_target="tpu_custom_call" | custom-call | flops 40000000000 | bytes 25000000 | tf_op jit(solution)/shard_map/attn_fwd/pallas_call | solution.py:86
  154.4 23.1 %add_convert_fusion.2 = bf16[2048,2048]{1,0:T(8,128)(2,1)S(1)} fusion(bf16[2048,2048]{1,0:T(8,128)(2,1)} %bitcast.87, bf16[2048,2048]{1,0:T(8,128)(2,1)} %get-tuple-element.27, bf16[2048,2048]{1,0:T(8,128)(2,1)} %bitcast.83), kind=kOutput, calls=%fused_computation.21 | convolution fusion | flops 17192452096 | bytes 33554432 | tf_op jit(solution)/shard_map/dot_general | solution.py:14
  177.6 69.9 %fusion.10 = (bf16[5632,2048]{1,0:T(8,128)(2,1)}, f32[2048,5632]{0,1:T(8,128)}) fusion(bf16[2048,2048]{1,0:T(8,128)(2,1)S(1)} %add_convert_fusion.2, bf16[2048,5632]{1,0:T(8,128)(2,1)} %param.14), kind=kOutput, calls=%fused_computation.15 | convolution fusion | flops 47348449280 | bytes 100663296 | tf_op jit(solution)/shard_map/dot_general | solution.py:14
  322.4 20.3 %collective-permute-done.7 = f32[704,2048]{1,0:T(8,128)S(1)} collective-permute-done((f32[704,2048]{1,0:T(8,128)S(1)}, f32[704,2048]{1,0:T(8,128)S(1)}, u32[]{:S(2)}, u32[]{:S(2)}) %collective-permute-start.7) | collective-permute-done | bytes 5767200 | tf_op jit(solution)/shard_map/ppermute | solution.py:194
  353.6 80.6 %fusion.2 = bf16[5632,2048]{1,0:T(8,128)(2,1)} fusion(f32[2048,5632]{0,1:T(8,128)} %get-tuple-element.82, bf16[5632,2048]{1,0:T(8,128)(2,1)} %param.15, bf16[2048,2048]{1,0:T(8,128)(2,1)} %bitcast), kind=kOutput, calls=%fused_computation.6 | convolution fusion | flops 47498395648 | bytes 100663296 | tf_op jit(solution)/shard_map/dot_general | solution.py:14
  493.2 66.1 %add_convert_fusion.1 = bf16[2048,2048]{1,0:T(8,128)(2,1)} fusion(bf16[2048,2048]{1,0:T(8,128)(2,1)} %bitcast, bf16[5632,2048]{1,0:T(8,128)(2,1)} %fusion.2, bf16[2048,5632]{1,0:T(8,128)(2,1)} %param.14), kind=kOutput, calls=%fused_computation.20 | convolution fusion | flops 47257223168 | bytes 62914560 | tf_op jit(solution)/shard_map/dot_general | solution.py:14
  559.8 19.9 %fusion.37 = f32[512,5632]{1,0:T(8,128)} fusion(bf16[5632,2048]{1,0:T(8,128)(2,1)} %fusion.2, bf16[2048,256]{1,0:T(8,128)(2,1)} %get-tuple-element.89, bf16[2048,256]{1,0:T(8,128)(2,1)S(1)} %get-tuple-element.88), kind=kOutput, calls=%fused_computation.76 | convolution fusion | flops 11815354368 | bytes 36700160 | tf_op jit(solution)/shard_map/dot_general | solution.py:14
  579.7 19.3 %fusion.33 = f32[512,5632]{1,0:T(8,128)} fusion(bf16[5632,2048]{1,0:T(8,128)(2,1)} %fusion.2, bf16[2048,256]{1,0:T(8,128)(2,1)S(1)} %get-tuple-element.83, bf16[2048,256]{1,0:T(8,128)(2,1)S(1)} %get-tuple-element.90), kind=kOutput, calls=%fused_computation.72 | convolution fusion | flops 11815354368 | bytes 36700160 | tf_op jit(solution)/shard_map/dot_general | solution.py:14
  599.0 21.5 %convolution_add_fusion = f32[512,5632]{1,0:T(8,128)} fusion(f32[512,5632]{1,0:T(8,128)} %fusion.37, bf16[5632,2048]{1,0:T(8,128)(2,1)} %collective-permute-done.12, bf16[2048,1024]{1,0:T(8,128)(2,1)} %collective-permute-done.11), kind=kOutput, calls=%fused_computation.22 | convolution fusion | flops 11814043648 | bytes 48234496 | tf_op jit(solution)/shard_map/dot_general | solution.py:14
  622.5 23.9 %convolution_convert_fusion.do_ref = bf16[2048,2048]{1,0:T(8,128)(2,1)} fusion(bf16[2048,2048]{1,0:T(8,128)(2,1)} %add_convert_fusion.1, bf16[2048,2048]{1,0:T(8,128)(2,1)} %bitcast.84), kind=kOutput, calls=%fused_computation.25 | convolution fusion | flops 17184063488 | bytes 25165824 | tf_op jit(solution)/shard_map/dot_general | solution.py:14
  663.2 21.8 %convolution_add_fusion.1 = f32[512,5632]{1,0:T(8,128)} fusion(f32[512,5632]{1,0:T(8,128)} %fusion.33, bf16[5632,2048]{1,0:T(8,128)(2,1)} %collective-permute-done.12, bf16[2048,1024]{1,0:T(8,128)(2,1)} %collective-permute-done.11), kind=kOutput, calls=%fused_computation.23 | convolution fusion | flops 11814043648 | bytes 48234496 | tf_op jit(solution)/shard_map/dot_general | solution.py:14
  706.7 41.2 %collective-permute-done.13 = f32[512,5632]{1,0:T(8,128)} collective-permute-done((f32[512,5632]{1,0:T(8,128)}, f32[512,5632]{1,0:T(8,128)}, u32[]{:S(2)}, u32[]{:S(2)}) %collective-permute-start.13) | collective-permute-done | bytes 11534368 | tf_op jit(solution)/shard_map/ppermute | solution.py:168
  757.6 126.7 %attn_bwd.1 = (bf16[2048,2048]{1,0:T(8,128)(2,1)}, f32[2048,256]{1,0:T(8,128)}, f32[2048,256]{1,0:T(8,128)}, f32[2048,256]{1,0:T(8,128)}, f32[2048,256]{1,0:T(8,128)}) custom-call(bf16[2048,2048]{1,0:T(8,128)(2,1)} %convolution_convert_fusion.1.q_ref, bf16[2048,512]{1,0:T(8,128)(2,1)} %copy-done.15, bf16[2048,512]{1,0:T(8,128)(2,1)} %collective-permute-done.k_oth.v_oth, ...), custom_call_target="tpu_custom_call" | custom-call | flops 99999997952 | bytes 40000000 | tf_op jit(solution)/shard_map/attn_bwd/pallas_call | solution.py:101
  897.2 25.5 %collective-permute-done.25 = f32[256,2048]{1,0:T(8,128)S(1)} collective-permute-done((f32[256,2048]{1,0:T(8,128)S(1)}, f32[256,2048]{1,0:T(8,128)S(1)}, u32[]{:S(2)}, u32[]{:S(2)}) %collective-permute-start.25) | collective-permute-done | bytes 2097184 | tf_op jit(solution)/shard_map/ppermute | solution.py:173
  985.2 67.4 %collective-permute-done.20 = f32[512,2048]{1,0:T(8,128)S(1)} collective-permute-done((f32[512,2048]{1,0:T(8,128)S(1)}, f32[512,2048]{1,0:T(8,128)S(1)}, u32[]{:S(2)}, u32[]{:S(2)}) %collective-permute-start.20) | collective-permute-done | bytes 4194336 | tf_op jit(solution)/shard_map/ppermute | solution.py:168
  1054.5 17.6 %collective-permute-done.23 = f32[128,2048]{1,0:T(8,128)S(1)} collective-permute-done((f32[128,2048]{1,0:T(8,128)S(1)}, f32[128,2048]{1,0:T(8,128)S(1)}, u32[]{:S(2)}, u32[]{:S(2)}) %collective-permute-start.23) | collective-permute-done | bytes 1048608 | tf_op jit(solution)/shard_map/ppermute | solution.py:168
  1074.7 17.2 %collective-permute-done.24 = f32[64,2048]{1,0:T(8,128)S(1)} collective-permute-done((f32[64,2048]{1,0:T(8,128)S(1)}, f32[64,2048]{1,0:T(8,128)S(1)}, u32[]{:S(2)}, u32[]{:S(2)}) %collective-permute-start.24) | collective-permute-done | bytes 524320 | tf_op jit(solution)/shard_map/ppermute | solution.py:173
  1095.6 26.1 %fusion.70 = f32[2048,2048]{1,0:T(8,128)} fusion(bf16[2048,2048]{1,0:T(8,128)(2,1)} %get-tuple-element.34, bf16[2048,2048]{1,0:T(8,128)(2,1)} %bitcast.95), kind=kOutput, calls=%fused_computation.152 | convolution fusion | flops 17179869184 | bytes 33554432 | tf_op jit(solution)/shard_map/dot_general | solution.py:14
  1150.4 45.9 %all-gather.5.cloned.1.call-done = f32[2560,2048]{1,0:T(8,128)} async-done(((f32[320,2048]{1,0:T(8,128)}), f32[2560,2048]{1,0:T(8,128)}) %all-gather.5.cloned.1.call-update) | async-done | bytes 20971536 | tf_op jit(solution)/shard_map/all_gather | solution.py:176
  1217.4 189.8 %all-gather.11.cloned.1.call-done = f32[5632,2048]{1,0:T(8,128)} async-done(((f32[704,2048]{1,0:T(8,128)}), f32[5632,2048]{1,0:T(8,128)}) %all-gather.11.cloned.1.call-update) | async-done | bytes 46137360 | tf_op jit(solution)/shard_map/all_gather | solution.py:176
  1407.2 34.1 %broadcast_multiply_fusion = f32[5632,2048]{1,0:T(8,128)} fusion(f32[5632,2048]{1,0:T(8,128)} %all-gather.11.cloned.1.call-done), kind=kLoop, calls=%fused_computation.16 | loop fusion | flops 11534336 | bytes 92274688 | tf_op jit(solution)/shard_map/mul | solution.py:239
  1441.3 177.2 %all-gather.9.cloned.1.call-done = f32[2048,5632]{1,0:T(8,128)} async-done(((f32[256,5632]{1,0:T(8,128)}), f32[2048,5632]{1,0:T(8,128)}) %all-gather.9.cloned.1.call-update) | async-done | bytes 46137360 | tf_op jit(solution)/shard_map/all_gather | solution.py:176
  1618.5 33.5 %broadcast_multiply_fusion.1 = f32[2048,5632]{1,0:T(8,128)} fusion(f32[2048,5632]{1,0:T(8,128)} %all-gather.9.cloned.1.call-done), kind=kLoop, calls=%fused_computation.17 | loop fusion | flops 11534336 | bytes 92274688 | tf_op jit(solution)/shard_map/mul | solution.py:240
  (147 shorter events, 337.9 us)
Async XLA Ops:
  7.2 1128.0 %all-gather.7.cloned.1.call-start = ((), (), s32[]{:S(2)}) async-start(), calls=%async_computation.1 | async-start | bytes 18874368 | tf_op jit(solution)/shard_map/all_gather | solution.py:176
  15.8 24.7 %collective-permute-start = (bf16[2048,512]{1,0:T(8,128)(2,1)S(1)}, bf16[2048,512]{1,0:T(8,128)(2,1)}, u32[]{:S(2)}, u32[]{:S(2)}) collective-permute-start(bf16[2048,512]{1,0:T(8,128)(2,1)S(1)} %fusion.20.k_own.v_own), channel_id=1, source_target_pairs={{0,1},{1,0},{2,3},{3,2},{4,5},{5,4},{6,7},{7,6}} | collective-permute-start | bytes 6291464 | tf_op jit(solution)/shard_map/ppermute | solution.py:126
  16.7 250.2 %collective-permute-start.2 = (bf16[2048,2048]{1,0:T(8,128)(2,1)}, bf16[2048,2048]{1,0:T(8,128)(2,1)}, u32[]{:S(2)}, u32[]{:S(2)}) collective-permute-start(bf16[2048,2048]{1,0:T(8,128)(2,1)} %bitcast), channel_id=1, source_target_pairs={{0,1},{1,0},{2,3},{3,2},{4,5},{5,4},{6,7},{7,6}} | collective-permute-start | bytes 25165832 | tf_op jit(solution)/shard_map/ppermute | solution.py:126
  266.8 34.1 %collective-permute-start.3 = (bf16[704,2048]{1,0:T(8,128)(2,1)S(1)}, bf16[704,2048]{1,0:T(8,128)(2,1)S(1)}, u32[]{:S(2)}, u32[]{:S(2)}) collective-permute-start(bf16[704,2048]{1,0:T(8,128)(2,1)S(1)} %copy-done.2), channel_id=1, source_target_pairs={{0,1},{1,0},{2,3},{3,2},{4,5},{5,4},{6,7},{7,6}} | collective-permute-start | bytes 8650760 | tf_op jit(solution)/shard_map/ppermute | solution.py:126
  276.4 66.3 %collective-permute-start.7 = (f32[704,2048]{1,0:T(8,128)S(1)}, f32[704,2048]{1,0:T(8,128)S(1)}, u32[]{:S(2)}, u32[]{:S(2)}) collective-permute-start(f32[704,2048]{1,0:T(8,128)S(1)} %convolution_add_fusion.2), channel_id=1, source_target_pairs={{0,2},{1,5},{2,0},{3,7},{4,6},{5,1},{6,4},{7,3}} | collective-permute-start | bytes 17301512 | tf_op jit(solution)/shard_map/ppermute | solution.py:194
  300.5 145.4 %collective-permute-start.1 = (bf16[704,2048]{1,0:T(8,128)(2,1)}, bf16[704,2048]{1,0:T(8,128)(2,1)}, u32[]{:S(2)}, u32[]{:S(2)}) collective-permute-start(bf16[704,2048]{1,0:T(8,128)(2,1)} %get-tuple-element.43), channel_id=1, source_target_pairs={{0,1},{1,0},{2,3},{3,2},{4,5},{5,4},{6,7},{7,6}} | collective-permute-start | bytes 8650760 | tf_op jit(solution)/shard_map/ppermute | solution.py:126
  311.3 145.8 %collective-permute-start.4 = (f32[704,2048]{1,0:T(8,128)}, f32[704,2048]{1,0:T(8,128)}, u32[]{:S(2)}, u32[]{:S(2)}) collective-permute-start(f32[704,2048]{1,0:T(8,128)} %convolution_add_fusion.3), channel_id=1, source_target_pairs={{0,2},{1,5},{2,0},{3,7},{4,6},{5,1},{6,4},{7,3}} | collective-permute-start | bytes 17301512 | tf_op jit(solution)/shard_map/ppermute | solution.py:195
  351.5 114.3 %collective-permute-start.8 = (f32[704,2048]{1,0:T(8,128)}, f32[704,2048]{1,0:T(8,128)}, u32[]{:S(2)}, u32[]{:S(2)}) collective-permute-start(f32[704,2048]{1,0:T(8,128)} %add_add_fusion), channel_id=1, source_target_pairs={{0,4},{1,3},{2,6},{3,1},{4,0},{5,7},{6,2},{7,5}} | collective-permute-start | bytes 17301512 | tf_op jit(solution)/shard_map/ppermute | solution.py:173
  445.9 153.1 %collective-permute-start.12 = (bf16[5632,2048]{1,0:T(8,128)(2,1)}, bf16[5632,2048]{1,0:T(8,128)(2,1)}, u32[]{:S(2)}, u32[]{:S(2)}) collective-permute-start(bf16[5632,2048]{1,0:T(8,128)(2,1)} %fusion.2), channel_id=1, source_target_pairs={{0,1},{1,0},{2,3},{3,2},{4,5},{5,4},{6,7},{7,6}} | collective-permute-start | bytes 69206024 | tf_op jit(solution)/shard_map/ppermute | solution.py:126
  490.4 108.6 %collective-permute-start.11 = (bf16[2048,1024]{1,0:T(8,128)(2,1)}, bf16[2048,1024]{1,0:T(8,128)(2,1)}, u32[]{:S(2)}, u32[]{:S(2)}) collective-permute-start(bf16[2048,1024]{1,0:T(8,128)(2,1)} %pad_maximum_fusion.1), channel_id=1, source_target_pairs={{0,1},{1,0},{2,3},{3,2},{4,5},{5,4},{6,7},{7,6}} | collective-permute-start | bytes 12582920 | tf_op jit(solution)/shard_map/ppermute | solution.py:126
  493.2 191.8 %collective-permute-start.9 = (bf16[2048,1024]{1,0:T(8,128)(2,1)}, bf16[2048,1024]{1,0:T(8,128)(2,1)}, u32[]{:S(2)}, u32[]{:S(2)}) collective-permute-start(bf16[2048,1024]{1,0:T(8,128)(2,1)} %pad_maximum_fusion), channel_id=1, source_target_pairs={{0,1},{1,0},{2,3},{3,2},{4,5},{5,4},{6,7},{7,6}} | collective-permute-start | bytes 12582920 | tf_op jit(solution)/shard_map/ppermute | solution.py:126
  559.4 125.7 %collective-permute-start.10 = (bf16[2048,2048]{1,0:T(8,128)(2,1)}, bf16[2048,2048]{1,0:T(8,128)(2,1)}, u32[]{:S(2)}, u32[]{:S(2)}) collective-permute-start(bf16[2048,2048]{1,0:T(8,128)(2,1)} %add_convert_fusion.1), channel_id=1, source_target_pairs={{0,1},{1,0},{2,3},{3,2},{4,5},{5,4},{6,7},{7,6}} | collective-permute-start | bytes 25165832 | tf_op jit(solution)/shard_map/ppermute | solution.py:126
  620.5 127.5 %collective-permute-start.13 = (f32[512,5632]{1,0:T(8,128)}, f32[512,5632]{1,0:T(8,128)}, u32[]{:S(2)}, u32[]{:S(2)}) collective-permute-start(f32[512,5632]{1,0:T(8,128)} %convolution_add_fusion), channel_id=1, source_target_pairs={{0,2},{1,5},{2,0},{3,7},{4,6},{5,1},{6,4},{7,3}} | collective-permute-start | bytes 34603016 | tf_op jit(solution)/shard_map/ppermute | solution.py:168
  754.1 130.3 %collective-permute-start.14 = (f32[512,2048]{1,0:T(8,128)}, f32[512,2048]{1,0:T(8,128)}, u32[]{:S(2)}, u32[]{:S(2)}) collective-permute-start(f32[512,2048]{1,0:T(8,128)} %convolution_add_fusion.7), channel_id=1, source_target_pairs={{0,2},{1,5},{2,0},{3,7},{4,6},{5,1},{6,4},{7,3}} | collective-permute-start | bytes 12582920 | tf_op jit(solution)/shard_map/ppermute | solution.py:168
  756.1 130.7 %collective-permute-start.15 = (f32[256,5632]{1,0:T(8,128)}, f32[256,5632]{1,0:T(8,128)}, u32[]{:S(2)}, u32[]{:S(2)}) collective-permute-start(f32[256,5632]{1,0:T(8,128)} %slice_add_fusion.1), channel_id=1, source_target_pairs={{0,4},{1,3},{2,6},{3,1},{4,0},{5,7},{6,2},{7,5}} | collective-permute-start | bytes 17301512 | tf_op jit(solution)/shard_map/ppermute | solution.py:173
  896.7 26.0 %collective-permute-start.25 = (f32[256,2048]{1,0:T(8,128)S(1)}, f32[256,2048]{1,0:T(8,128)S(1)}, u32[]{:S(2)}, u32[]{:S(2)}) collective-permute-start(f32[256,2048]{1,0:T(8,128)S(1)} %slice_add_fusion.5), channel_id=1, source_target_pairs={{0,4},{1,3},{2,6},{3,1},{4,0},{5,7},{6,2},{7,5}} | collective-permute-start | bytes 6291464 | tf_op jit(solution)/shard_map/ppermute | solution.py:173
  926.8 269.5 %all-gather.5.cloned.1.call-start = ((), (), s32[]{:S(2)}) async-start(), calls=%async_computation | async-start | bytes 23592960 | tf_op jit(solution)/shard_map/all_gather | solution.py:176
  926.9 35.1 %collective-permute-start.19 = (bf16[2048,2048]{1,0:T(8,128)(2,1)}, bf16[2048,2048]{1,0:T(8,128)(2,1)}, u32[]{:S(2)}, u32[]{:S(2)}) collective-permute-start(bf16[2048,2048]{1,0:T(8,128)(2,1)} %bitcast.88), channel_id=1, source_target_pairs={{0,1},{1,0},{2,3},{3,2},{4,5},{5,4},{6,7},{7,6}} | collective-permute-start | bytes 25165832 | tf_op jit(solution)/shard_map/ppermute | solution.py:126
  936.3 25.7 %collective-permute-start.18 = (bf16[2048,1024]{1,0:T(8,128)(2,1)}, bf16[2048,1024]{1,0:T(8,128)(2,1)}, u32[]{:S(2)}, u32[]{:S(2)}) collective-permute-start(bf16[2048,1024]{1,0:T(8,128)(2,1)} %pad_maximum_fusion.2), channel_id=1, source_target_pairs={{0,1},{1,0},{2,3},{3,2},{4,5},{5,4},{6,7},{7,6}} | collective-permute-start | bytes 12582920 | tf_op jit(solution)/shard_map/ppermute | solution.py:126
  970.4 82.2 %collective-permute-start.20 = (f32[512,2048]{1,0:T(8,128)S(1)}, f32[512,2048]{1,0:T(8,128)S(1)}, u32[]{:S(2)}, u32[]{:S(2)}) collective-permute-start(f32[512,2048]{1,0:T(8,128)S(1)} %convolution_add_fusion.4), channel_id=1, source_target_pairs={{0,2},{1,5},{2,0},{3,7},{4,6},{5,1},{6,4},{7,3}} | collective-permute-start | bytes 12582920 | tf_op jit(solution)/shard_map/ppermute | solution.py:168
  972.7 99.3 %collective-permute-start.23 = (f32[128,2048]{1,0:T(8,128)S(1)}, f32[128,2048]{1,0:T(8,128)S(1)}, u32[]{:S(2)}, u32[]{:S(2)}) collective-permute-start(f32[128,2048]{1,0:T(8,128)S(1)} %slice.130), channel_id=1, source_target_pairs={{0,2},{1,5},{2,0},{3,7},{4,6},{5,1},{6,4},{7,3}} | collective-permute-start | bytes 3145736 | tf_op jit(solution)/shard_map/ppermute | solution.py:168
  1053.0 39.1 %collective-permute-start.21 = (f32[256,2048]{1,0:T(8,128)S(1)}, f32[256,2048]{1,0:T(8,128)S(1)}, u32[]{:S(2)}, u32[]{:S(2)}) collective-permute-start(f32[256,2048]{1,0:T(8,128)S(1)} %slice_add_fusion.3), channel_id=1, source_target_pairs={{0,4},{1,3},{2,6},{3,1},{4,0},{5,7},{6,2},{7,5}} | collective-permute-start | bytes 6291464 | tf_op jit(solution)/shard_map/ppermute | solution.py:173
  1094.3 312.9 %all-gather.11.cloned.1.call-start = ((), (), s32[]{:S(2)}) async-start(), calls=%async_computation.3 | async-start | bytes 51904512 | tf_op jit(solution)/shard_map/all_gather | solution.py:176
  1095.0 523.4 %all-gather.9.cloned.1.call-start = ((), (), s32[]{:S(2)}) async-start(), calls=%async_computation.2 | async-start | bytes 51904512 | tf_op jit(solution)/shard_map/all_gather | solution.py:176
  (28 other events, 594.5 us)
Sparse Core Ops, SparseCore 0:
  926.9 100.4 all-gather.6
  1094.4 101.8 all-gather.4
  1198.2 208.9 all-gather.10
  1409.5 208.9 all-gather.8
